TPU v7x, 8 devices: a whole 2x2x1 slice. The times are simulated.
8 devices in a mesh: dp: 1 (over z), tp: 2 (over y), sp: 4 (over x, core).
Axes of the slice: x: 2, y: 2, z: 1, core: 2. Of those that a mesh axis runs over, the one named last changes fastest.
Arguments:
- hidden: bfloat16 [512, 2048], P('dp')
- ln_gain: bfloat16 [2048], replicated
- ln_bias: bfloat16 [2048], replicated
- w_q: bfloat16 [2048, 2048], P(None, 'tp')
- w_k: bfloat16 [2048, 512], P(None, 'tp')
- w_v: bfloat16 [2048, 512], P(None, 'tp')
- w_o: bfloat16 [2048, 2048], P('tp')
- k_cache: bfloat16 [512, 1024, 8, 64], P('dp', 'sp', 'tp')
- v_cache: bfloat16 [512, 1024, 8, 64], P('dp', 'sp', 'tp')
- lengths: int32 [512], P('dp')
Outputs:
- output 1: bfloat16 [512, 2048], P('dp')
- output 2: bfloat16 [512, 8, 64], P('dp', 'tp')
- output 3: bfloat16 [512, 8, 64], P('dp', 'tp')
All inputs are finite; a program needn't handle non-finite values.
Results may differ from a plain program's by a relative error of at most 0.00379527.
Values sent between devices are 32-bit elements.
A program may use at most 1 GiB of HBM per device.

v0:
```python
import jax
import jax.numpy as jnp
from jax import lax
from jax.sharding import PartitionSpec as P, NamedSharding


def norm_one_plus(hidden, ln_gain, ln_bias):
    wide = hidden.astype(jnp.float32)
    row_mean = jnp.mean(wide, axis=-1, keepdims=True)
    centred = wide - row_mean
    row_var = jnp.mean(centred * centred, axis=-1, keepdims=True)
    scaled = centred * lax.rsqrt(row_var + 1e-5)
    return (scaled * (1.0 + ln_gain.astype(jnp.float32)) + ln_bias.astype(jnp.float32)).astype(jnp.bfloat16)


def rotate_first(head_vecs, rot_pos, rot_dim):
    half_rot = rot_dim // 2
    inv_freq = 10000.0 ** (-2.0 * jnp.arange(half_rot, dtype=jnp.float32) / rot_dim)
    rot_angle = rot_pos.astype(jnp.float32)[..., None] * inv_freq
    cos_part = jnp.cos(rot_angle)
    sin_part = jnp.sin(rot_angle)
    lead_part = head_vecs[..., :half_rot]
    tail_part = head_vecs[..., half_rot:rot_dim]
    return jnp.concatenate([lead_part * cos_part - tail_part * sin_part, tail_part * cos_part + lead_part * sin_part, head_vecs[..., rot_dim:]], axis=-1)


def solution(mesh):
    def local_step(hidden, ln_gain, ln_bias, w_q, w_k, w_v, w_o, k_cache, v_cache, lengths):
        batch_rows, seq_local, kv_local, head_dim = k_cache.shape
        group_size = w_q.shape[1] // (head_dim * kv_local)
        rot_dim = head_dim // 2
        score_scale = head_dim ** -0.5
        normed = norm_one_plus(hidden, ln_gain, ln_bias)
        q_proj = jnp.dot(normed, w_q, preferred_element_type=jnp.float32).reshape(batch_rows, kv_local, group_size, head_dim)
        queries = rotate_first(q_proj, lengths[:, None, None], rot_dim).astype(jnp.bfloat16)
        k_proj = jnp.dot(normed, w_k, preferred_element_type=jnp.float32).reshape(batch_rows, kv_local, head_dim)
        k_new = rotate_first(k_proj, lengths[:, None], rot_dim).astype(jnp.bfloat16)
        v_new = jnp.dot(normed, w_v, preferred_element_type=jnp.float32).astype(jnp.bfloat16).reshape(batch_rows, kv_local, head_dim)
        block_index = lax.axis_index('sp')
        positions = block_index * seq_local + jnp.arange(seq_local)
        valid = positions[None, :] < lengths[:, None]
        scores = jnp.einsum('bkgd,bskd->bkgs', queries, k_cache, preferred_element_type=jnp.float32) * score_scale
        scores = jnp.where(valid[:, None, None, :], scores, -jnp.inf)
        owner = (lengths // seq_local) == block_index
        self_score = jnp.einsum('clhe,cle->clh', queries, k_new, preferred_element_type=jnp.float32) * score_scale
        self_score = jnp.where(owner[:, None, None], self_score, -jnp.inf)
        block_max = jnp.maximum(jnp.max(scores, axis=-1), self_score)
        safe_max = jnp.where(jnp.isfinite(block_max), block_max, 0.0)
        weights = jnp.exp(scores - safe_max[..., None])
        self_weight = jnp.exp(self_score - safe_max)
        weight_sum = jnp.sum(weights, axis=-1) + self_weight
        weighted = jnp.einsum('bkgs,bskd->bkgd', weights.astype(jnp.bfloat16), v_cache, preferred_element_type=jnp.float32)
        weighted = weighted + self_weight[..., None] * v_new.astype(jnp.float32)[:, :, None, :]
        packed = jnp.concatenate([weighted, block_max[..., None], weight_sum[..., None]], axis=-1)
        gathered = lax.all_gather(packed, 'sp', axis=0)
        all_max = gathered[..., head_dim]
        global_max = jnp.max(all_max, axis=0)
        factor = jnp.exp(all_max - global_max)
        total = jnp.sum(gathered[..., head_dim + 1] * factor, axis=0)
        context = jnp.sum(gathered[..., :head_dim] * factor[..., None], axis=0) / total[..., None]
        context = context.astype(jnp.bfloat16).reshape(batch_rows, kv_local * group_size * head_dim)
        partial_out = jnp.dot(context, w_o, preferred_element_type=jnp.float32)
        summed = lax.psum(partial_out, 'tp')
        out = (hidden.astype(jnp.float32) + summed).astype(jnp.bfloat16)
        return out, k_new, v_new

    row_spec = P('dp', None)
    cache_spec = P('dp', 'sp', 'tp', None)
    head_spec = P('dp', 'tp', None)
    return jax.shard_map(local_step, mesh=mesh, in_specs=(row_spec, P(None), P(None), P(None, 'tp'), P(None, 'tp'), P(None, 'tp'), P('tp', None), cache_spec, cache_spec, P('dp')), out_specs=(row_spec, head_spec, head_spec), check_vma=False)
```

profile of v0, /device:TPU:1, one launch (start us, length us, event | category | flops | bytes accessed | tf_op | source)
XLA Modules:
  0.0 368.3 jit_solution(6205553313213694622)
XLA Ops:
  7.2 0.0 copy-start
  7.2 0.0 copy-start.2
  7.2 0.0 copy-start.8
  7.2 0.0 copy-start.9
  7.2 0.0 all-gather.3.cloned.1.call-start
  7.3 0.8 convert_element_type.48
  8.1 2.0 convert_reduce_fusion
  10.1 2.3 fusion.8
  12.5 0.8 fusion.11
  13.3 0.0 copy-start.6
  13.3 0.8 fusion.31
  14.1 1.2 copy-done.10
  15.3 2.4 fusion.30
  17.8 0.2 multiply_cosine_fusion
  18.0 1.0 subtract_convert_fusion
  19.0 0.9 slice.68
  19.9 0.1 broadcast_compare_fusion
  20.0 3.3 convolution_convert_fusion
  23.4 2.2 copy.104
  25.6 1.3 pad_maximum_fusion.1
  26.8 2.9 copy.92
  29.8 2.2 copy.93
  31.9 5.2 %fusion.32 = f32[512,4,1,4]{3,2,1,0:T(1,128)} fusion(bf16[512,4,4,64]{3,2,1,0:T(4,128)(2,1)} %copy.92, bf16[512,4,64,1]{2,3,1,0:T(2,128)(2,1)} %copy.104), kind=kOutput, calls=%fused_computation.68 | convolution fusion | flops 1048576 | bytes 1343488 | tf_op jit(solution)/shard_map/clhe,cle->clh/dot_general | solution.py:45
  37.2 27.2 %fusion.1 = (f32[512,4,4]{2,1,0:T(4,128)S(1)}, f32[512,4,4,256]{3,2,1,0:T(4,128)}) fusion(pred[512,256]{1,0:T(8,128)(4,1)S(1)} %broadcast_compare_fusion, bf16[512,4,4,64]{3,2,1,0:T(4,128)(2,1)} %copy.92, bf16[512,256,4,64]{1,3,2,0:T(8,128)(2,1)} %param.17), kind=kOutput, calls=%fused_computation.4 | convolution fusion | flops 274718720 | bytes 76709888 | tf_op jit(solution)/shard_map/bkgd,bskd->bkgs/dot_general | solution.py:42
  64.4 4.0 %fusion.29 = (f32[512,4,4,1]{2,1,0,3:T(4,128)}, f32[512,4,4]{2,1,0:T(4,128)S(1)}) fusion(f32[512,4,4]{2,1,0:T(4,128)S(1)} %get-tuple-element.13, f32[512,4,4]{2,1,0:T(4,128)} %bitcast.42, pred[512]{0:T(512)(128)(4,1)S(1)} %fusion.25), kind=kLoop, calls=%fused_computation.65 | loop fusion | flops 40960 | bytes 131584 | tf_op jit(solution)/shard_map/broadcast_in_dim | solution.py:54
  68.4 15.9 %fusion.4 = f32[512,4,4]{2,1,0:T(4,128)S(1)} fusion(f32[512,4,4,256]{3,2,1,0:T(4,128)} %get-tuple-element.14, f32[512,4,4]{2,1,0:T(4,128)S(1)} %get-tuple-element.8, pred[512,256]{1,0:T(8,128)(4,1)S(1)} %broadcast_compare_fusion), kind=kLoop, calls=%fused_computation.10 | loop fusion | flops 8380416 | bytes 8585216 | tf_op jit(solution)/shard_map/reduce_sum | solution.py:51
  84.4 3.0 add_bitcast_fusion
  87.4 14.4 %copy.97 = f32[512,4,4,1]{3,2,1,0:T(4,128)} copy(f32[512,4,4,1]{2,1,0,3:T(4,128)} %get-tuple-element.3) | data formatting | bytes 65536 | tf_op jit(solution)/shard_map/broadcast_in_dim | solution.py:54
  101.8 13.5 %copy.96 = f32[512,4,4,1]{3,2,1,0:T(4,128)} copy(f32[512,4,4,1]{2,1,0,3:T(4,128)S(1)} %copy-done.3) | data formatting | bytes 65536 | tf_op jit(solution)/shard_map/broadcast_in_dim | solution.py:54
  115.3 29.6 %multiply_add_fusion = f32[512,4,4,64]{3,2,1,0:T(4,128)} fusion(bf16[512,256,4,64]{1,3,2,0:T(8,128)(2,1)} %param.18, f32[512,4,4,256]{3,2,1,0:T(4,128)} %get-tuple-element.14, f32[512,4,4]{2,1,0:T(4,128)} %copy-done.5, pred[512,256]{1,0:T(8,128)(4,1)S(1)} %broadcast_compare_fusion, f32[512,4,64]{2,1,0:T(4,128)} %copy.93, f32[512,4,4]{2,1,0:T(4,128)} %get-tuple-element.4), kind=kOutput, calls=%fused_computation.19 | convolution fusion | flops 277872640 | bytes 78315520 | tf_op jit(solution)/shard_map/bkgs,bskd->bkgd/dot_general | solution.py:52
  144.8 8.6 %pad_maximum_fusion = f32[512,4,4,66]{3,2,1,0:T(4,128)} fusion(f32[512,4,4,1]{3,2,1,0:T(4,128)} %copy.97, f32[512,4,4,1]{3,2,1,0:T(4,128)} %copy.96, f32[512,4,4,64]{3,2,1,0:T(4,128)} %multiply_add_fusion), kind=kLoop, calls=%fused_computation.18 | loop fusion | flops 1081344 | bytes 4325376 | tf_op jit(solution)/shard_map/concatenate | solution.py:54
  153.5 6.8 %copy.98 = f32[512,4,4,66]{0,2,3,1:T(4,128)} copy(f32[512,4,4,66]{3,2,1,0:T(4,128)} %pad_maximum_fusion) | data formatting | bytes 4325376 | tf_op jit(solution)/shard_map/concatenate | solution.py:54
  160.3 0.0 all-gather.3.cloned.1.call-update
  160.3 0.0 all-reduce.2.cloned.1.call-start
  160.4 59.6 %all-gather.3.cloned.1.call-done = f32[2048,4,4,66]{0,2,3,1:T(4,128)} async-done(((f32[512,4,4,66]{0,2,3,1:T(4,128)}), f32[2048,4,4,66]{0,2,3,1:T(4,128)}) %all-gather.3.cloned.1.call-update) | async-done | bytes 8650768 | tf_op jit(solution)/shard_map/all_gather | solution.py:55
  219.9 12.0 %reshape.196 = f32[4,512,4,4,66]{1,0,3,4,2:T(4,128)} reshape(f32[2048,4,4,66]{0,2,3,1:T(4,128)} %all-gather.3.cloned.1.call-done) | data formatting | bytes 17301504 | tf_op jit(solution)/shard_map/all_gather | solution.py:55
  231.9 1.0 slice_reduce_fusion
  232.9 1.7 fusion.22
  234.6 1.0 exponential_bitcast_fusion
  235.6 11.3 %fusion = f32[512,4,4,64]{0,2,3,1:T(4,128)} fusion(f32[4,512,4,4,66]{1,0,3,4,2:T(4,128)} %reshape.196, f32[4,512,4,4]{1,0,3,2:T(4,128)S(1)} %exponential_bitcast_fusion), kind=kLoop, calls=%fused_computation.1 | loop fusion | flops 3670016 | bytes 10616832 | tf_op jit(solution)/shard_map/reduce_sum | solution.py:60
  246.9 2.2 fusion.19
  249.1 6.5 %fusion.33 = f32[512,2048]{1,0:T(8,128)} fusion(bf16[512,1024]{0,1:T(8,128)(2,1)S(1)} %bitcast.41, bf16[1024,2048]{1,0:T(8,128)(2,1)} %param.16), kind=kOutput, calls=%fused_computation.69 | convolution fusion | flops 2147483648 | bytes 9437184 | tf_op jit(solution)/shard_map/dot_general | solution.py:62
  255.6 0.0 all-reduce.2.cloned.1.call-update
  255.6 0.0 copy-start.1
  255.7 0.7 pad_maximum_fusion.2
  256.4 100.8 %all-reduce.2.cloned.1.call-done = f32[512,2048]{1,0:T(8,128)} async-done(((f32[512,2048]{1,0:T(8,128)}), f32[512,2048]{1,0:T(8,128)}) %all-reduce.2.cloned.1.call-update) | async-done | bytes 4194320 | tf_op jit(solution)/shard_map/psum | solution.py:63
  357.2 4.2 %fusion.12 = bf16[512,2048]{1,0:T(8,128)(2,1)} fusion(f32[512,2048]{1,0:T(8,128)} %all-reduce.2.cloned.1.call-done, bf16[512,2048]{1,0:T(8,128)(2,1)S(1)} %copy-done.2), kind=kLoop, calls=%fused_computation.17 | loop fusion | flops 3145728 | bytes 8388608 | tf_op jit(solution)/shard_map/convert_element_type | solution.py:64
  361.4 0.0 copy-done.1
  (24 shorter events, 0.1 us)
Async XLA Ops:
  7.2 6.1 %copy-start = (bf16[2048,256]{1,0:T(8,128)(2,1)S(1)}, bf16[2048,256]{1,0:T(8,128)(2,1)}, u32[]{:S(2)}) copy-start(bf16[2048,256]{1,0:T(8,128)(2,1)} %param.14) | copy-start | bytes 3145732
  7.2 5.3 %copy-start.2 = (bf16[512,2048]{1,0:T(8,128)(2,1)S(1)}, bf16[512,2048]{1,0:T(8,128)(2,1)}, u32[]{:S(2)}) copy-start(bf16[512,2048]{1,0:T(8,128)(2,1)} %param.10) | copy-start | bytes 6291460
  7.2 5.2 %copy-start.8 = (bf16[2048]{0:T(1024)(128)(2,1)S(1)}, bf16[2048]{0:T(1024)(128)(2,1)}, u32[]{:S(2)}) copy-start(bf16[2048]{0:T(1024)(128)(2,1)} %param.11) | copy-start | bytes 12292
  7.2 5.2 %copy-start.9 = (bf16[2048]{0:T(1024)(128)(2,1)S(1)}, bf16[2048]{0:T(1024)(128)(2,1)}, u32[]{:S(2)}) copy-start(bf16[2048]{0:T(1024)(128)(2,1)} %param.12) | copy-start | bytes 12292
  7.2 212.7 %all-gather.3.cloned.1.call-start = ((), (), s32[]{:S(2)}) async-start(), calls=%async_computation.1 | async-start | bytes 10813440 | tf_op jit(solution)/shard_map/all_gather | solution.py:55
  12.4 3.0 copy-start.10
  13.3 4.4 %copy-start.6 = (bf16[512,2048]{1,0:T(8,128)(2,1)}, bf16[512,2048]{1,0:T(8,128)(2,1)S(1)}, u32[]{:S(2)}) copy-start(bf16[512,2048]{1,0:T(8,128)(2,1)S(1)} %fusion.11) | copy-start | bytes 6291460
  15.3 4.5 %copy-start.7 = (s32[512]{0:T(512)S(1)}, s32[512]{0:T(512)}, u32[]{:S(2)}) copy-start(s32[512]{0:T(512)} %param.19) | copy-start | bytes 6148
  68.4 15.9 %copy-start.5 = (f32[512,4,4]{2,1,0:T(4,128)}, f32[512,4,4]{2,1,0:T(4,128)S(1)}, u32[]{:S(2)}) copy-start(f32[512,4,4]{2,1,0:T(4,128)S(1)} %get-tuple-element.8) | copy-start | bytes 98308
  68.4 16.0 %copy-start.4 = (f32[512,4,1,4]{3,2,1,0:T(1,128)S(1)}, f32[512,4,1,4]{3,2,1,0:T(1,128)}, u32[]{:S(2)}) copy-start(f32[512,4,1,4]{3,2,1,0:T(1,128)} %fusion.32) | copy-start | bytes 98308
  87.4 14.4 %copy-start.3 = (f32[512,4,4,1]{2,1,0,3:T(4,128)S(1)}, f32[512,4,4,1]{2,1,0,3:T(4,128)}, u32[]{:S(2)}) copy-start(f32[512,4,4,1]{2,1,0,3:T(4,128)} %get-tuple-element.7) | copy-start | bytes 98308
  160.3 196.9 %all-reduce.2.cloned.1.call-start = ((), (), s32[]{:S(2)}) async-start(), calls=%async_computation | async-start | bytes 8388608 | tf_op jit(solution)/shard_map/psum | solution.py:63
  255.6 105.8 %copy-start.1 = (bf16[2048,256]{1,0:T(8,128)(2,1)S(1)}, bf16[2048,256]{1,0:T(8,128)(2,1)}, u32[]{:S(2)}) copy-start(bf16[2048,256]{1,0:T(8,128)(2,1)} %param.14) | copy-start | bytes 3145732
Sparse Core Ops, SparseCore 0:
  160.4 59.4 all-gather.2
  255.8 101.3 all-reduce.1
where the time goes:
time: 370 us; the launch traced here: 368 us
  waiting for transfers between devices  160 us (43%)
  matrix products  75.1 us (20%)
  other arithmetic  62.3 us (17%)
  local copies, waits for them, and re-layouts  56.1 us (15%)
  between operations  14.3 us (4%)
    psum x1, waiting for transfers between devices, local_step(): summed = lax.psum(partial_out, 'tp')  101 us
    all_gather x1, waiting for transfers between devices, local_step(): gathered = lax.all_gather(packed, 'sp', axis=0)  59.6 us
    dot_general x1, matrix products, local_step(): jnp.einsum('bkgs,bskd->bkgd', weights.astype(jnp.bfloat16), v_cache, pref...  29.6 us
    dot_general x1, matrix products, local_step(): jnp.einsum('bkgd,bskd->bkgs', queries, k_cache, preferred_element_type=jn...  27.2 us
    reduce_sum x1, other arithmetic, local_step(): weight_sum = jnp.sum(weights, axis=-1) + self_weight  15.9 us
    broadcast_in_dim x1, local copies, waits for them, and re-layouts, local_step(): weight_sum[..., None]  14.4 us
    broadcast_in_dim x1, local copies, waits for them, and re-layouts, local_step(): block_max[..., None]  13.5 us
    all_gather x1, local copies, waits for them, and re-layouts, local_step(): gathered = lax.all_gather(packed, 'sp', axis=0)  12 us
  transfers between devices with their start and end apart: 2, of which 2 were waited for; matrix products, arithmetic and copies ran while one was open for 0% of the time, Pallas kernels for 0%

commit v1 on v0

v1 whole, which is shorter than its diff:
```python
import functools

import jax
import jax.numpy as jnp
import numpy as np
from jax import lax
from jax.experimental import pallas as pl
from jax.experimental.pallas import tpu as pltpu
from jax.sharding import PartitionSpec as P

MESH = pl.DeviceIdType.MESH
F32 = jnp.float32
BF16 = jnp.bfloat16
LOWEST = float(jnp.finfo(jnp.float32).min)

GROUP = 16
BLOCK = 4 * GROUP + 8
CHUNKS = (4, 8, 8, 8, 4)
SLOTS = 7
LAGS = (0, 2, 6, 10, 15, 17)
PITCH = 520


def attention_kernel(len_sm, len_row, inv_freq, gain, bias, hid_hbm, wq_hbm, wk_hbm, wv_hbm, wo_hbm, k_hbm, v_hbm,
                     out_hbm, knt_ref, vnt_ref,
                     hid, wq, wk, wv, wo, kring, vring, stage, cos_t, sin_t, qx, kn, vn,
                     own, part, send2, mine, recv2, ctx, proj, recv3, total,
                     ring_sem, load_sem, out_sem, send_sem, recv_sem):
    rows, width = hid.shape
    groups = rows // GROUP
    span = k_hbm.shape[2]
    tp = lax.axis_index('tp')
    sp = lax.axis_index('sp')
    x, core = sp // 2, sp % 2

    def ring_copy(g, slot):
        src = pl.ds(g * GROUP, GROUP)
        return (pltpu.make_async_copy(k_hbm.at[src], kring.at[slot], ring_sem.at[slot, 0]),
                pltpu.make_async_copy(v_hbm.at[src], vring.at[slot], ring_sem.at[slot, 1]))

    load_hid = pltpu.make_async_copy(hid_hbm, hid, load_sem.at[0])
    load_wk = pltpu.make_async_copy(wk_hbm, wk, load_sem.at[1])
    load_wv = pltpu.make_async_copy(wv_hbm, wv, load_sem.at[2])
    load_wq = pltpu.make_async_copy(wq_hbm, wq, load_sem.at[3])
    load_wo = pltpu.make_async_copy(wo_hbm, wo, load_sem.at[4])
    load_hid.start()
    load_wk.start()
    load_wv.start()
    load_wq.start()
    for g in range(SLOTS):
        for copy in ring_copy(g, g):
            copy.start()
    load_wo.start()

    def device(dx, dcore, dtp):
        return {'sp': (x ^ dx) * 2 + (core ^ dcore), 'tp': tp ^ dtp}

    barrier = pltpu.get_barrier_semaphore()
    for peer in ((0, 1, 0), (1, 0, 0), (0, 0, 1), (1, 0, 1)):
        pl.semaphore_signal(barrier, inc=1, device_id=device(*peer), device_id_type=MESH)

    angle = inv_freq[:, 0:1] * len_row[0:1, :].astype(F32)
    cos_a, sin_a = jnp.cos(angle), jnp.sin(angle)
    one, zero = jnp.ones((32, rows), F32), jnp.zeros((32, rows), F32)
    cos_full = jnp.concatenate([cos_a, cos_a, one] * 2, axis=0)
    sin_full = jnp.concatenate([-sin_a, sin_a, zero] * 2, axis=0)
    for blk in range(rows // 128):
        cut = slice(blk * 128, blk * 128 + 128)
        cos_t[cut, :] = cos_full[:, cut].T
        sin_t[cut, :] = sin_full[:, cut].T

    load_hid.wait()
    gain_f = 1.0 + gain[...].astype(F32)
    bias_f = bias[...].astype(F32)

    def norm(i, _):
        at = pl.ds(pl.multiple_of(i * 16, 16), 16)
        wide = hid[at, :].astype(F32)
        centred = wide - jnp.mean(wide, axis=-1, keepdims=True)
        var = jnp.mean(centred * centred, axis=-1, keepdims=True)
        stage[at, :] = (centred * lax.rsqrt(var + 1e-5) * gain_f + bias_f).astype(BF16)
        return 0

    lax.fori_loop(0, rows // 16, norm, 0)

    load_wk.wait()
    load_wv.wait()
    load_wq.wait()
    lane_rb = lax.broadcasted_iota(jnp.int32, (128, 128), 1)
    low_half = lane_rb < 64
    first_rot = (lane_rb % 64) < 16

    def rotate(u, cos_b, sin_b):
        partner = jnp.where(first_rot, pltpu.roll(u, 112, 1), pltpu.roll(u, 16, 1))
        return (u * cos_b + partner * sin_b).astype(BF16).astype(F32)

    def project(i, _):
        start = pl.multiple_of(i * 128, 128)
        at = pl.ds(start, 128)
        normed = stage[at, :]
        cos_b, sin_b = cos_t[at, :], sin_t[at, :]
        for head in range(4):
            q = jnp.dot(normed, wq[:, head * 256:head * 256 + 256], preferred_element_type=F32)
            for j in range(2):
                u = rotate(q[:, j * 128:j * 128 + 128], cos_b, sin_b) * 0.125
                swap = pltpu.roll(u, 64, 1)
                if head % 2 == 0:
                    a, b = jnp.where(low_half, u, 0.0), jnp.where(low_half, swap, 0.0)
                else:
                    a, b = jnp.where(low_half, 0.0, swap), jnp.where(low_half, 0.0, u)
                r = head * 4 + 2 * j
                qx[pl.ds(pl.multiple_of(r * PITCH + start, 8), 128), :] = a
                qx[pl.ds(pl.multiple_of((r + 1) * PITCH + start, 8), 128), :] = b
        kp = jnp.dot(normed, wk[...], preferred_element_type=F32)
        vp = jnp.dot(normed, wv[...], preferred_element_type=F32)
        for j in range(2):
            cut = slice(j * 128, j * 128 + 128)
            ku = rotate(kp[:, cut], cos_b, sin_b)
            vu = vp[:, cut].astype(BF16).astype(F32)
            kn[at, cut] = ku
            vn[at, cut] = vu
            knt_ref[cut, at] = ku.T.astype(BF16)
            vnt_ref[cut, at] = vu.T.astype(BF16)
        return 0

    lax.fori_loop(0, rows // 128, project, 0)
    pl.semaphore_wait(barrier, 4)

    lane = lax.broadcasted_iota(jnp.int32, (8, 128), 1)
    row = lax.broadcasted_iota(jnp.int32, (8, 128), 0)
    low = lane < 64
    keep_w = (row < 4) == low
    stat = lane % 8
    even = (lane % 2) == 0
    keep_s = (row < 4) == even
    pair_of = lane // 8
    pos = lax.broadcasted_iota(jnp.int32, (16, span), 1)
    zero8 = jnp.zeros((8, 128), F32)
    first_pos = sp * span

    def pack(a, b, pick, keep):
        same = jnp.where(pick, a, b)
        other = pltpu.roll(jnp.where(pick, b, a), 4, 0)
        return jnp.where(keep, same, other)

    def one_sequence(b, keys, values):
        qa = qx[pl.ds(b, 8, stride=PITCH), :]
        qb = qx[pl.ds(b + 8 * PITCH, 8, stride=PITCH), :]
        q = jnp.concatenate([jnp.concatenate([qa, zero8], 1), jnp.concatenate([zero8, qb], 1)], 0).astype(BF16)
        s = jnp.dot(q, keys, preferred_element_type=F32)
        left = len_sm[b] - first_pos
        s = jnp.where(pos < left, s, -jnp.inf)
        k_self, v_self = kn[pl.ds(b, 1), :], vn[pl.ds(b, 1), :]
        s_self = jnp.sum(jnp.concatenate([qa * k_self[:, :128], qb * k_self[:, 128:]], 0), axis=1, keepdims=True)
        owner = jnp.logical_and(left >= 0, left < span)
        s_self = s_self + jnp.where(owner, 0.0, -jnp.inf)
        top = jnp.maximum(jnp.maximum(jnp.max(s, axis=1, keepdims=True), s_self), LOWEST)
        w = jnp.exp(s - top)
        w_self = jnp.exp(s_self - top)
        denom = jnp.sum(w, axis=1, keepdims=True) + w_self
        ctx_b = lax.dot_general(w.astype(BF16), values, (((1,), (1,)), ((), ())), preferred_element_type=F32)
        ca = ctx_b[:8, :128] + w_self[:8] * v_self[:, :128]
        cb = ctx_b[8:, 128:] + w_self[8:] * v_self[:, 128:]
        stats = jnp.where(stat < 2, top[:8], jnp.where(stat < 4, top[8:], jnp.where(stat < 6, denom[:8], denom[8:])))
        return ca, cb, stats

    def attend(g, slot):
        tile = zero8
        for p in range(GROUP // 2):
            b = g * GROUP + 2 * p
            e = one_sequence(b, kring[slot, 2 * p], vring[slot, 2 * p])
            o = one_sequence(b + 1, kring[slot, 2 * p + 1], vring[slot, 2 * p + 1])
            own[g, 8 * p:8 * p + 8, 0:128] = pack(e[0], o[0], low, keep_w)
            own[g, 8 * p:8 * p + 8, 128:256] = pack(e[1], o[1], low, keep_w)
            tile = jnp.where(pair_of == p, pack(e[2], o[2], even, keep_s), tile)
        own[g, 4 * GROUP:BLOCK, 0:128] = tile
        own[g, 4 * GROUP:BLOCK, 128:256] = zero8

    is_top = stat < 4

    def spread(f, p, t):
        c = p * 8 + 2 * t
        return jnp.where(low, jnp.broadcast_to(f[:, c:c + 1], (8, 128)), jnp.broadcast_to(f[:, c + 1:c + 2], (8, 128)))

    def merge(a_ref, a, b_ref, b, emit):
        sa, sb = a_ref[a, 4 * GROUP:BLOCK, 0:128], b_ref[b, 4 * GROUP:BLOCK, 0:128]
        top = jnp.maximum(sa, sb)
        fa, fb = jnp.exp(sa - top), jnp.exp(sb - top)
        denom = sa * pltpu.roll(fa, 4, 1) + sb * pltpu.roll(fb, 4, 1)
        emit(None, None, jnp.where(is_top, top, denom))
        for p in range(GROUP // 2):
            r = slice(8 * p, 8 * p + 8)
            for t in range(2):
                c = slice(t * 128, t * 128 + 128)
                w = a_ref[a, r, c] * spread(fa, p, t) + b_ref[b, r, c] * spread(fb, p, t)
                emit(r, c, w / spread(denom, p, 2 + t) if emit.final else w)

    def store_to(ref, index, final):
        def emit(r, c, value):
            if r is None:
                if not final:
                    ref[index, 4 * GROUP:BLOCK, 0:128] = value
                    ref[index, 4 * GROUP:BLOCK, 128:256] = zero8
            elif final:
                base = c.start // 128 * (ref.shape[0] // 2)
                ref[pl.ds(pl.multiple_of(base + index * 4 * GROUP + r.start, 8), 8), :] = value
            else:
                ref[index, r, c] = value
        emit.final = final
        return emit

    starts = [sum(CHUNKS[:c]) for c in range(len(CHUNKS))]

    def remote(c, kind, src, dst, peer):
        return pltpu.make_async_remote_copy(
            src_ref=src, dst_ref=dst, send_sem=send_sem.at[c, kind], recv_sem=recv_sem.at[c, kind],
            device_id=device(*peer), device_id_type=MESH)

    def quarter(c):
        return CHUNKS[c] // 4

    def to_partner(c):
        n = quarter(c)
        src = own.at[pl.ds(starts[c] + (1 - core) * 2 * n, 2 * n)]
        return remote(c, 0, src, part.at[pl.ds(starts[c] // 2, 2 * n)], (0, 1, 0))

    def over_x(c):
        at = pl.ds(starts[c] // 4, quarter(c))
        return remote(c, 1, send2.at[at], recv2.at[at], (1, 0, 0))

    def over_y(c):
        half = quarter(c) * GROUP // 2
        src = proj.at[pl.ds(pl.multiple_of(starts[c] // 4 * GROUP + (1 - tp) * half, 8), half)]
        return remote(c, 2, src, recv3.at[pl.ds(starts[c] // 4 * GROUP // 2, half)], (0, 0, 1))

    def home(c, dx, dcore, dtp):
        half = quarter(c) * GROUP // 2
        index = ((core ^ dcore) * 2 + (x ^ dx)) * 2 + (tp ^ dtp)
        return total.at[pl.ds(pl.multiple_of(starts[c] * GROUP + index * half, 8), half)]

    def spread_own(c, kind, peer):
        return remote(c, kind, home(c, 0, 0, 0), home(c, 0, 0, 0), peer)

    def forward(c, kind, origin):
        return remote(c, kind, home(c, *origin), home(c, *origin), (0, 1, 0))

    direct = ((3, (0, 1, 0)), (4, (1, 0, 0)), (5, (0, 0, 1)), (6, (1, 0, 1)))
    passed = ((7, (1, 0, 0)), (8, (0, 0, 1)), (9, (1, 0, 1)))

    def step1(c):
        to_partner(c).start()

    def step2(c):
        n = quarter(c)
        to_partner(c).wait_recv()
        for dx in (1, 0):
            side = x ^ dx

            def body(i, _):
                out = (send2, mine)[1 - dx]
                merge(own, starts[c] + (core * 2 + side) * n + i, part, starts[c] // 2 + side * n + i,
                      store_to(out, starts[c] // 4 + i, False))
                return 0

            lax.fori_loop(0, n, body, 0)
            if dx == 1:
                over_x(c).start()

    def step3(c):
        n = quarter(c)
        if c == 0:
            load_wo.wait()
        over_x(c).wait_recv()

        def body(i, _):
            at = starts[c] // 4 + i
            merge(mine, at, recv2, at, store_to(ctx, i, True))
            return 0

        lax.fori_loop(0, n, body, 0)
        m = n * GROUP
        side = ctx.shape[0] // 2
        lhs = [jnp.concatenate([ctx[pl.ds(t * side + g, m, stride=4), :] for t in range(2)], 1).astype(BF16) for g in range(4)]
        for col in range(width // 256):
            cut = slice(col * 256, col * 256 + 256)
            acc = None
            for g in range(4):
                rhs = jnp.concatenate([wo[h * 256 + g * 64:h * 256 + g * 64 + 64, cut] for h in range(4)], 0)
                term = jnp.dot(lhs[g], rhs, preferred_element_type=F32)
                acc = term if acc is None else acc + term
            proj[starts[c] // 4 * GROUP:starts[c] // 4 * GROUP + m, cut] = acc
        over_y(c).start()

    def step4(c):
        half = quarter(c) * GROUP // 2
        over_y(c).wait_recv()
        src = pl.ds(pl.multiple_of(starts[c] // 4 * GROUP + tp * half, 8), half)
        other = starts[c] // 4 * GROUP // 2
        home(c, 0, 0, 0)[...] = proj[src, :] + recv3[other:other + half, :]
        for kind, peer in direct:
            spread_own(c, kind, peer).start()

    def step5(c):
        for (kind, origin), (arrived, _) in zip(passed, direct[1:]):
            spread_own(c, arrived, (0, 1, 0)).wait_recv()
            forward(c, kind, origin).start()

    def out_copy(c):
        at = pl.ds(starts[c] * GROUP, CHUNKS[c] * GROUP)
        return pltpu.make_async_copy(stage.at[at], out_hbm.at[at], out_sem.at[c])

    def step6(c):
        spread_own(c, 3, (0, 1, 0)).wait_recv()
        for kind, origin in passed:
            forward(c, kind, origin).wait_recv()

        def body(i, _):
            at = pl.ds(pl.multiple_of((starts[c] + i) * GROUP, GROUP), GROUP)
            stage[at, :] = (hid[at, :].astype(F32) + total[at, :]).astype(BF16)
            return 0

        lax.fori_loop(0, CHUNKS[c], body, 0)
        out_copy(c).start()

    steps = (step1, step2, step3, step4, step5, step6)
    events = sorted((starts[c] + CHUNKS[c] - 1 + LAGS[i], c, i) for c in range(len(CHUNKS)) for i in range(6))

    def loop(g, _):
        slot = lax.rem(g, SLOTS)
        for copy in ring_copy(g, slot):
            copy.wait()
        attend(g, slot)

        @pl.when(g + SLOTS < groups)
        def _():
            for copy in ring_copy(g + SLOTS, slot):
                copy.start()

        for when, c, i in events:
            if when < groups:
                pl.when(g == when)(functools.partial(steps[i], c))
        return 0

    lax.fori_loop(0, groups, loop, 0)
    for when, c, i in events:
        if when >= groups:
            steps[i](c)
    for c in range(len(CHUNKS)):
        to_partner(c).wait_send()
        over_x(c).wait_send()
        over_y(c).wait_send()
        for kind, peer in direct:
            spread_own(c, kind, peer).wait_send()
        for kind, origin in passed:
            forward(c, kind, origin).wait_send()
        out_copy(c).wait()


def solution(mesh):
    def local_step(hidden, ln_gain, ln_bias, w_q, w_k, w_v, w_o, k_cache, v_cache, lengths):
        rows, span, kv_local, head_dim = k_cache.shape
        width = hidden.shape[1]
        kv_width = kv_local * head_dim
        q_width = w_q.shape[1]
        groups = rows // GROUP
        keys = jnp.transpose(k_cache, (0, 2, 3, 1)).reshape(rows, kv_width, span)
        values = jnp.transpose(v_cache, (0, 2, 3, 1)).reshape(rows, kv_width, span)
        half_rot = head_dim // 4
        inv_freq = np.power(10000.0, -2.0 * np.arange(half_rot) / (2 * half_rot)).astype(np.float32)
        inv_freq = jnp.asarray(np.broadcast_to(inv_freq[:, None], (half_rot, 128)).copy())
        vmem = pl.BlockSpec(memory_space=pltpu.VMEM)
        smem = pl.BlockSpec(memory_space=pltpu.SMEM)
        hbm = pl.BlockSpec(memory_space=pl.ANY)
        n = len(CHUNKS)
        out, k_new, v_new = pl.pallas_call(
            attention_kernel,
            out_shape=(jax.ShapeDtypeStruct((rows, width), BF16),
                       jax.ShapeDtypeStruct((kv_width, rows), BF16),
                       jax.ShapeDtypeStruct((kv_width, rows), BF16)),
            in_specs=[smem, vmem, vmem, vmem, vmem] + [hbm] * 7,
            out_specs=(hbm, vmem, vmem),
            scratch_shapes=[
                pltpu.VMEM((rows, width), BF16),
                pltpu.VMEM((width, q_width), BF16),
                pltpu.VMEM((width, kv_width), BF16),
                pltpu.VMEM((width, kv_width), BF16),
                pltpu.VMEM((q_width, width), BF16),
                pltpu.VMEM((SLOTS, GROUP, kv_width, span), BF16),
                pltpu.VMEM((SLOTS, GROUP, kv_width, span), BF16),
                pltpu.VMEM((rows, width), BF16),
                pltpu.VMEM((rows, 128), F32),
                pltpu.VMEM((rows, 128), F32),
                pltpu.VMEM((16 * PITCH, 128), F32),
                pltpu.VMEM((rows, kv_width), F32),
                pltpu.VMEM((rows, kv_width), F32),
                pltpu.VMEM((groups, BLOCK, 256), F32),
                pltpu.VMEM((groups // 2, BLOCK, 256), F32),
                pltpu.VMEM((groups // 4, BLOCK, 256), F32),
                pltpu.VMEM((groups // 4, BLOCK, 256), F32),
                pltpu.VMEM((groups // 4, BLOCK, 256), F32),
                pltpu.VMEM((2 * (max(CHUNKS) // 4) * GROUP * 4, 128), F32),
                pltpu.VMEM((rows // 4, width), F32),
                pltpu.VMEM((rows // 8, width), F32),
                pltpu.VMEM((rows, width), F32),
                pltpu.SemaphoreType.DMA((SLOTS, 2)),
                pltpu.SemaphoreType.DMA((5,)),
                pltpu.SemaphoreType.DMA((n,)),
                pltpu.SemaphoreType.DMA((n, 10)),
                pltpu.SemaphoreType.DMA((n, 10)),
            ],
            compiler_params=pltpu.CompilerParams(
                collective_id=0, has_side_effects=True, vmem_limit_bytes=67043328),
        )(lengths, lengths.reshape(1, rows), inv_freq, ln_gain.reshape(1, width), ln_bias.reshape(1, width),
          hidden, w_q, w_k, w_v, w_o, keys, values)
        k_new = jnp.transpose(k_new.reshape(kv_local, head_dim, rows), (2, 0, 1))
        v_new = jnp.transpose(v_new.reshape(kv_local, head_dim, rows), (2, 0, 1))
        return out, k_new, v_new

    row_spec = P('dp', None)
    cache_spec = P('dp', 'sp', 'tp', None)
    head_spec = P('dp', 'tp', None)
    return jax.shard_map(local_step, mesh=mesh, in_specs=(row_spec, P(None), P(None), P(None, 'tp'), P(None, 'tp'), P(None, 'tp'), P('tp', None), cache_spec, cache_spec, P('dp')), out_specs=(row_spec, head_spec, head_spec), check_vma=False)
```

time: 370 us -> 131 us (0.35)
  waiting for transfers between devices: 160 us -> 0 us
  Pallas kernels: 0 us -> 123 us
  matrix products: 75.1 us -> 0 us
  other arithmetic: 62.3 us -> 0 us
  local copies, waits for them, and re-layouts: 56.1 us -> 7.21 us
  between operations: 14.3 us -> 0.66 us
    pallas_call x0 -> x1, Pallas kernels: none -> 123 us  [local_step(): pl.pallas_call(attention_kernel, out_shape=(jax.ShapeDtypeStruct((rows, w...]
    psum x1 -> x0, waiting for transfers between devices: 101 us -> none  [local_step(): summed = lax.psum(partial_out, 'tp')]
    dot_general x7 -> x0, matrix products: 75.1 us -> none  [the longest x1 29.6 us: local_step(): jnp.einsum('bkgs,bskd->bkgd', weights.astype(jnp.bfloat16), v_cache, pref...]
    all_gather x1 -> x0, waiting for transfers between devices: 59.6 us -> none  [local_step(): gathered = lax.all_gather(packed, 'sp', axis=0)]
    reduce_sum x5 -> x0, other arithmetic: 33.2 us -> none  [the longest x1 15.9 us: local_step(): weight_sum = jnp.sum(weights, axis=-1) + self_weight]
    broadcast_in_dim x2 -> x0, local copies, waits for them, and re-layouts: 27.9 us -> none  [the longest x1 14.4 us: local_step(): weight_sum[..., None]]
    all_gather x1 -> x0, local copies, waits for them, and re-layouts: 12 us -> none  [local_step(): gathered = lax.all_gather(packed, 'sp', axis=0)]
    concatenate x3 -> x0, local copies, waits for them, and re-layouts: 11.9 us -> none  [the longest x1 6.83 us: local_step(): jnp.concatenate([weighted, block_max[..., None], weight_sum[..., None]],...]
  transfers between devices with their start and end apart: 2 -> 0, of which waited for: 2 -> 0; matrix products, arithmetic and copies ran while one was open for 0% -> 0% of each run, Pallas kernels for 0% -> 0%
where the time goes in v1:
time: 131 us
  Pallas kernels  123 us (94%)
  local copies, waits for them, and re-layouts  7.21 us (6%)
    pallas_call x1, Pallas kernels, local_step(): pl.pallas_call(attention_kernel, out_shape=(jax.ShapeDtypeStruct((rows, w...  123 us
    unnamed x7, local copies, waits for them, and re-layouts  4.63 us

profile of v1, /device:TPU:1, one launch (start us, length us, event | category | flops | bytes accessed | tf_op | source)
XLA Modules:
  0.0 130.8 jit_solution(8845676272421369383)
XLA Ops:
  0.6 1.3 reshape.28.gain
  1.9 1.3 reshape.29.bias
  3.2 122.9 %shard_map.130 = (bf16[512,2048]{1,0:T(8,128)(2,1)}, bf16[256,512]{1,0:T(8,128)(2,1)}, bf16[256,512]{1,0:T(8,128)(2,1)}) custom-call(s32[512]{0:T(512)} %len_sm.1, s32[1,512]{1,0:T(1,128)} %bitcast.15, f32[16,128]{1,0:T(8,128)} %constant.2.clone.inv_freq, bf16[1,2048]{1,0:T(2,128)(2,1)} %reshape.28.gain, bf16[1,2048]{1,0:T(2,128)(2,1)} %reshape.29.bias, ...), custom_call_target="tpu_custom_call" | custom-call | tf_op jit(solution)/shard_map/pallas_call | solution.py:375
  126.1 0.0 copy-start.1
  126.1 0.0 copy-start
  126.2 3.2 %copy.17 = bf16[512,2048]{1,0:T(8,128)(2,1)} copy(bf16[512,2048]{1,0:T(8,128)(2,1)} %get-tuple-element.12) | data formatting | bytes 4194304
  129.4 0.0 copy-done.1
  129.4 0.7 copy.18
  130.1 0.0 copy-done
  130.1 0.7 copy.19
Async XLA Ops:
  126.1 3.2 %copy-start.1 = (bf16[256,512]{1,0:T(8,128)(2,1)S(1)}, bf16[256,512]{1,0:T(8,128)(2,1)}, u32[]{:S(2)}) copy-start(bf16[256,512]{1,0:T(8,128)(2,1)} %get-tuple-element.7) | copy-start | bytes 786436
  126.1 3.9 %copy-start = (bf16[256,512]{1,0:T(8,128)(2,1)S(1)}, bf16[256,512]{1,0:T(8,128)(2,1)}, u32[]{:S(2)}) copy-start(bf16[256,512]{1,0:T(8,128)(2,1)} %get-tuple-element.8) | copy-start | bytes 786436

commit v2 on v1

--- a/solution.py
+++ b/solution.py
@@ -1,4 +1,5 @@
 import functools
+import math
 
 import jax
 import jax.numpy as jnp
@@ -15,16 +16,17 @@
 
 GROUP = 16
 BLOCK = 4 * GROUP + 8
-CHUNKS = (4, 8, 8, 8, 4)
+DIRECT = (3, 4)
+CHUNKS = (8, 8, 8, 4, 4)
 SLOTS = 7
-LAGS = (0, 2, 6, 10, 15, 17)
+LAGS = (0, 0.9, 2.9, 4.8, 6.8, 7.7, 8.6)
 PITCH = 520
 
 
 def attention_kernel(len_sm, len_row, inv_freq, gain, bias, hid_hbm, wq_hbm, wk_hbm, wv_hbm, wo_hbm, k_hbm, v_hbm,
                      out_hbm, knt_ref, vnt_ref,
                      hid, wq, wk, wv, wo, kring, vring, stage, cos_t, sin_t, qx, kn, vn,
-                     own, part, send2, mine, recv2, ctx, proj, recv3, total,
+                     prob, self_w, own, part, send2, mine, recv2, ctx, proj, recv3, total,
                      ring_sem, load_sem, out_sem, send_sem, recv_sem):
     rows, width = hid.shape
     groups = rows // GROUP
@@ -33,24 +35,28 @@
     sp = lax.axis_index('sp')
     x, core = sp // 2, sp % 2
 
-    def ring_copy(g, slot):
-        src = pl.ds(g * GROUP, GROUP)
-        return (pltpu.make_async_copy(k_hbm.at[src], kring.at[slot], ring_sem.at[slot, 0]),
-                pltpu.make_async_copy(v_hbm.at[src], vring.at[slot], ring_sem.at[slot, 1]))
-
-    load_hid = pltpu.make_async_copy(hid_hbm, hid, load_sem.at[0])
-    load_wk = pltpu.make_async_copy(wk_hbm, wk, load_sem.at[1])
-    load_wv = pltpu.make_async_copy(wv_hbm, wv, load_sem.at[2])
-    load_wq = pltpu.make_async_copy(wq_hbm, wq, load_sem.at[3])
-    load_wo = pltpu.make_async_copy(wo_hbm, wo, load_sem.at[4])
-    load_hid.start()
+    def ring_copy(which, g):
+        slot = lax.rem(g, SLOTS)
+        src, ring = ((k_hbm, kring), (v_hbm, vring))[which]
+        return pltpu.make_async_copy(src.at[pl.ds(g * GROUP, GROUP)], ring.at[slot], ring_sem.at[slot, which])
+
+    blocks = rows // 128
+
+    def load_hid(i):
+        at = pl.ds(i * 128, 128)
+        return pltpu.make_async_copy(hid_hbm.at[at], hid.at[at], load_sem.at[4 + i])
+
+    load_wk = pltpu.make_async_copy(wk_hbm, wk, load_sem.at[0])
+    load_wv = pltpu.make_async_copy(wv_hbm, wv, load_sem.at[1])
+    load_wq = pltpu.make_async_copy(wq_hbm, wq, load_sem.at[2])
+    load_wo = pltpu.make_async_copy(wo_hbm, wo, load_sem.at[3])
+    for i in range(blocks):
+        load_hid(i).start()
+    load_wq.start()
     load_wk.start()
     load_wv.start()
-    load_wq.start()
-    for g in range(SLOTS):
-        for copy in ring_copy(g, g):
-            copy.start()
-    load_wo.start()
+    for which in range(2):
+        ring_copy(which, 0).start()
 
     def device(dx, dcore, dtp):
         return {'sp': (x ^ dx) * 2 + (core ^ dcore), 'tp': tp ^ dtp}
@@ -69,23 +75,33 @@
         cos_t[cut, :] = cos_full[:, cut].T
         sin_t[cut, :] = sin_full[:, cut].T
 
-    load_hid.wait()
-    gain_f = 1.0 + gain[...].astype(F32)
-    bias_f = bias[...].astype(F32)
+    with jax.named_scope('load_hid'):
+        for i in range(blocks):
+            load_hid(i).wait()
+    for g in range(1, SLOTS):
+        for which in range(2):
+            ring_copy(which, g).start()
+    load_wo.start()
+    gain_f, bias_f = gain[...].astype(F32), bias[...].astype(F32)
+    gain_f = 1.0 + jnp.concatenate([gain_f[i:i + 1] for i in range(width // 128)], 1)
+    bias_f = jnp.concatenate([bias_f[i:i + 1] for i in range(width // 128)], 1)
 
     def norm(i, _):
-        at = pl.ds(pl.multiple_of(i * 16, 16), 16)
-        wide = hid[at, :].astype(F32)
-        centred = wide - jnp.mean(wide, axis=-1, keepdims=True)
-        var = jnp.mean(centred * centred, axis=-1, keepdims=True)
-        stage[at, :] = (centred * lax.rsqrt(var + 1e-5) * gain_f + bias_f).astype(BF16)
+        for j in range(4):
+            at = pl.ds(pl.multiple_of(i * 64 + j * 16, 16), 16)
+            wide = hid[at, :].astype(F32)
+            centred = wide - jnp.mean(wide, axis=-1, keepdims=True)
+            var = jnp.mean(centred * centred, axis=-1, keepdims=True)
+            stage[at, :] = (centred * lax.rsqrt(var + 1e-5) * gain_f + bias_f).astype(BF16)
         return 0
 
-    lax.fori_loop(0, rows // 16, norm, 0)
-
-    load_wk.wait()
-    load_wv.wait()
-    load_wq.wait()
+    with jax.named_scope('norm'):
+        lax.fori_loop(0, rows // 64, norm, 0)
+
+    with jax.named_scope('load_w'):
+        load_wk.wait()
+        load_wv.wait()
+        load_wq.wait()
     lane_rb = lax.broadcasted_iota(jnp.int32, (128, 128), 1)
     low_half = lane_rb < 64
     first_rot = (lane_rb % 64) < 16
@@ -123,8 +139,10 @@
             vnt_ref[cut, at] = vu.T.astype(BF16)
         return 0
 
-    lax.fori_loop(0, rows // 128, project, 0)
-    pl.semaphore_wait(barrier, 4)
+    with jax.named_scope('project'):
+        lax.fori_loop(0, rows // 128, project, 0)
+    with jax.named_scope('barrier'):
+        pl.semaphore_wait(barrier, 4)
 
     lane = lax.broadcasted_iota(jnp.int32, (8, 128), 1)
     row = lax.broadcasted_iota(jnp.int32, (8, 128), 0)
@@ -143,14 +161,22 @@
         other = pltpu.roll(jnp.where(pick, b, a), 4, 0)
         return jnp.where(keep, same, other)
 
-    def one_sequence(b, keys, values):
+    def queries(b):
         qa = qx[pl.ds(b, 8, stride=PITCH), :]
         qb = qx[pl.ds(b + 8 * PITCH, 8, stride=PITCH), :]
+        return qa, qb
+
+    def score(g, j):
+        qa, qb = queries(g * GROUP + j)
         q = jnp.concatenate([jnp.concatenate([qa, zero8], 1), jnp.concatenate([zero8, qb], 1)], 0).astype(BF16)
-        s = jnp.dot(q, keys, preferred_element_type=F32)
+        return jnp.dot(q, kring[lax.rem(g, SLOTS), j], preferred_element_type=F32)
+
+    def weigh(g, side, j, s):
+        b = g * GROUP + j
+        qa, qb = queries(b)
         left = len_sm[b] - first_pos
         s = jnp.where(pos < left, s, -jnp.inf)
-        k_self, v_self = kn[pl.ds(b, 1), :], vn[pl.ds(b, 1), :]
+        k_self = kn[pl.ds(b, 1), :]
         s_self = jnp.sum(jnp.concatenate([qa * k_self[:, :128], qb * k_self[:, 128:]], 0), axis=1, keepdims=True)
         owner = jnp.logical_and(left >= 0, left < span)
         s_self = s_self + jnp.where(owner, 0.0, -jnp.inf)
@@ -158,23 +184,36 @@
         w = jnp.exp(s - top)
         w_self = jnp.exp(s_self - top)
         denom = jnp.sum(w, axis=1, keepdims=True) + w_self
-        ctx_b = lax.dot_general(w.astype(BF16), values, (((1,), (1,)), ((), ())), preferred_element_type=F32)
-        ca = ctx_b[:8, :128] + w_self[:8] * v_self[:, :128]
-        cb = ctx_b[8:, 128:] + w_self[8:] * v_self[:, 128:]
-        stats = jnp.where(stat < 2, top[:8], jnp.where(stat < 4, top[8:], jnp.where(stat < 6, denom[:8], denom[8:])))
-        return ca, cb, stats
-
-    def attend(g, slot):
-        tile = zero8
+        prob[side, 16 * j:16 * j + 16, :] = w.astype(BF16)
+        self_w[side, 16 * j:16 * j + 16, :] = jnp.broadcast_to(w_self, (16, 128))
+        return jnp.where(stat < 2, top[:8], jnp.where(stat < 4, top[8:], jnp.where(stat < 6, denom[:8], denom[8:])))
+
+    def value(g, side, j):
+        v_self = vn[pl.ds(g * GROUP + j, 1), :]
+        part_b = lax.dot_general(prob[side, 16 * j:16 * j + 16, :], vring[lax.rem(g, SLOTS), j],
+                                 (((1,), (1,)), ((), ())), preferred_element_type=F32)
+        ca = part_b[:8, :128] + self_w[side, 16 * j:16 * j + 8, :] * v_self[:, :128]
+        cb = part_b[8:, 128:] + self_w[side, 16 * j + 8:16 * j + 16, :] * v_self[:, 128:]
+        return ca, cb
+
+    def attend(score_g, value_g):
+        if score_g is not None:
+            g, side = score_g
+            scores = [score(g, j) for j in range(GROUP)]
+            tile = zero8
         for p in range(GROUP // 2):
-            b = g * GROUP + 2 * p
-            e = one_sequence(b, kring[slot, 2 * p], vring[slot, 2 * p])
-            o = one_sequence(b + 1, kring[slot, 2 * p + 1], vring[slot, 2 * p + 1])
-            own[g, 8 * p:8 * p + 8, 0:128] = pack(e[0], o[0], low, keep_w)
-            own[g, 8 * p:8 * p + 8, 128:256] = pack(e[1], o[1], low, keep_w)
-            tile = jnp.where(pair_of == p, pack(e[2], o[2], even, keep_s), tile)
-        own[g, 4 * GROUP:BLOCK, 0:128] = tile
-        own[g, 4 * GROUP:BLOCK, 128:256] = zero8
+            if value_g is not None:
+                v, vside = value_g
+                e, o = value(v, vside, 2 * p), value(v, vside, 2 * p + 1)
+                own[v, 8 * p:8 * p + 8, 0:128] = pack(e[0], o[0], low, keep_w)
+                own[v, 8 * p:8 * p + 8, 128:256] = pack(e[1], o[1], low, keep_w)
+            if score_g is not None:
+                e = weigh(g, side, 2 * p, scores[2 * p])
+                o = weigh(g, side, 2 * p + 1, scores[2 * p + 1])
+                tile = jnp.where(pair_of == p, pack(e, o, even, keep_s), tile)
+        if score_g is not None:
+            own[g, 4 * GROUP:BLOCK, 0:128] = tile
+            own[g, 4 * GROUP:BLOCK, 128:256] = zero8
 
     is_top = stat < 4
 
@@ -244,15 +283,25 @@
     def forward(c, kind, origin):
         return remote(c, kind, home(c, *origin), home(c, *origin), (0, 1, 0))
 
-    direct = ((3, (0, 1, 0)), (4, (1, 0, 0)), (5, (0, 0, 1)), (6, (1, 0, 1)))
     passed = ((7, (1, 0, 0)), (8, (0, 0, 1)), (9, (1, 0, 1)))
+    first_peer, other_peer = (1 - core, 0, core), (core, 0, 1 - core)
+
+    def sent(c):
+        copies = [spread_own(c, 4, (1, 0, 0)), spread_own(c, 5, (0, 0, 1)), spread_own(c, 3, (0, 1, 0))]
+        if c in DIRECT:
+            copies.append(spread_own(c, 6, (1, 0, 1)))
+        return copies
+
+    def relay(c):
+        return remote(c, 6, home(c, *first_peer), home(c, *first_peer), other_peer)
 
     def step1(c):
         to_partner(c).start()
 
     def step2(c):
         n = quarter(c)
-        to_partner(c).wait_recv()
+        with jax.named_scope(f'wait2_{c}'):
+            to_partner(c).wait_recv()
         for dx in (1, 0):
             side = x ^ dx
 
@@ -270,7 +319,8 @@
         n = quarter(c)
         if c == 0:
             load_wo.wait()
-        over_x(c).wait_recv()
+        with jax.named_scope(f'wait3_{c}'):
+            over_x(c).wait_recv()
 
         def body(i, _):
             at = starts[c] // 4 + i
@@ -293,26 +343,38 @@
 
     def step4(c):
         half = quarter(c) * GROUP // 2
-        over_y(c).wait_recv()
+        with jax.named_scope(f'wait4_{c}'):
+            over_y(c).wait_recv()
         src = pl.ds(pl.multiple_of(starts[c] // 4 * GROUP + tp * half, 8), half)
         other = starts[c] // 4 * GROUP // 2
         home(c, 0, 0, 0)[...] = proj[src, :] + recv3[other:other + half, :]
-        for kind, peer in direct:
-            spread_own(c, kind, peer).start()
+        for copy in sent(c):
+            copy.start()
 
     def step5(c):
-        for (kind, origin), (arrived, _) in zip(passed, direct[1:]):
-            spread_own(c, arrived, (0, 1, 0)).wait_recv()
-            forward(c, kind, origin).start()
+        with jax.named_scope(f'wait5_{c}'):
+            spread_own(c, 4 + core, (0, 1, 0)).wait_recv()
+        if c not in DIRECT:
+            relay(c).start()
+        forward(c, 7 + core, first_peer).start()
+
+    def step6(c):
+        with jax.named_scope(f'wait6a_{c}'):
+            spread_own(c, 5 - core, (0, 1, 0)).wait_recv()
+        forward(c, 8 - core, other_peer).start()
+        with jax.named_scope(f'wait6b_{c}'):
+            spread_own(c, 6, (0, 1, 0)).wait_recv()
+        forward(c, 9, (1, 0, 1)).start()
 
     def out_copy(c):
         at = pl.ds(starts[c] * GROUP, CHUNKS[c] * GROUP)
         return pltpu.make_async_copy(stage.at[at], out_hbm.at[at], out_sem.at[c])
 
-    def step6(c):
-        spread_own(c, 3, (0, 1, 0)).wait_recv()
-        for kind, origin in passed:
-            forward(c, kind, origin).wait_recv()
+    def step7(c):
+        with jax.named_scope(f'wait7_{c}'):
+            spread_own(c, 3, (0, 1, 0)).wait_recv()
+            for kind, origin in passed:
+                forward(c, kind, origin).wait_recv()
 
         def body(i, _):
             at = pl.ds(pl.multiple_of((starts[c] + i) * GROUP, GROUP), GROUP)
@@ -322,38 +384,68 @@
         lax.fori_loop(0, CHUNKS[c], body, 0)
         out_copy(c).start()
 
-    steps = (step1, step2, step3, step4, step5, step6)
-    events = sorted((starts[c] + CHUNKS[c] - 1 + LAGS[i], c, i) for c in range(len(CHUNKS)) for i in range(6))
-
-    def loop(g, _):
-        slot = lax.rem(g, SLOTS)
-        for copy in ring_copy(g, slot):
-            copy.wait()
-        attend(g, slot)
-
+    def scoped(i, c):
+        with jax.named_scope(f'step{i + 1}_{c}'):
+            steps[i](c)
+
+    steps = (step1, step2, step3, step4, step5, step6, step7)
+    events = sorted(((starts[c] + CHUNKS[c]) / 2 - 1 + LAGS[i], c, i) for c in range(len(CHUNKS)) for i in range(7))
+
+    def wait_for(keys, values):
+        for g in keys:
+            ring_copy(0, g).wait()
+        for g in values:
+            ring_copy(1, g).wait()
+
+    def refill(which, g):
         @pl.when(g + SLOTS < groups)
         def _():
-            for copy in ring_copy(g + SLOTS, slot):
-                copy.start()
-
-        for when, c, i in events:
-            if when < groups:
-                pl.when(g == when)(functools.partial(steps[i], c))
+            ring_copy(which, g + SLOTS).start()
+
+    wait_for((0,), ())
+    with jax.named_scope('attend'):
+        attend((0, 0), None)
+    refill(0, 0)
+
+    def loop(i, _):
+        g = 2 * i
+        with jax.named_scope('ring_wait'):
+            wait_for((g + 1, g + 2), (g, g + 1))
+        with jax.named_scope('attend'):
+            attend((g + 1, 1), (g, 0))
+            attend((g + 2, 0), (g + 1, 1))
+        refill(0, g + 1)
+        refill(1, g)
+        refill(0, g + 2)
+        refill(1, g + 1)
+        for when, c, k in events:
+            if when <= trips - 1:
+                pl.when(i == math.ceil(when))(functools.partial(scoped, k, c))
         return 0
 
-    lax.fori_loop(0, groups, loop, 0)
-    for when, c, i in events:
-        if when >= groups:
-            steps[i](c)
-    for c in range(len(CHUNKS)):
-        to_partner(c).wait_send()
-        over_x(c).wait_send()
-        over_y(c).wait_send()
-        for kind, peer in direct:
-            spread_own(c, kind, peer).wait_send()
-        for kind, origin in passed:
-            forward(c, kind, origin).wait_send()
-        out_copy(c).wait()
+    trips = groups // 2 - 1
+    lax.fori_loop(0, trips, loop, 0)
+    last = groups - 2
+    with jax.named_scope('ring_wait'):
+        wait_for((last + 1,), (last, last + 1))
+    with jax.named_scope('attend'):
+        attend((last + 1, 1), (last, 0))
+        attend(None, (last + 1, 1))
+    for when, c, k in events:
+        if when > trips - 1:
+            scoped(k, c)
+    with jax.named_scope('finish'):
+        for c in range(len(CHUNKS)):
+            to_partner(c).wait_send()
+            over_x(c).wait_send()
+            over_y(c).wait_send()
+            for copy in sent(c):
+                copy.wait_send()
+            if c not in DIRECT:
+                relay(c).wait_send()
+            for kind, origin in passed:
+                forward(c, kind, origin).wait_send()
+            out_copy(c).wait()
 
 
 def solution(mesh):
@@ -393,6 +485,8 @@
                 pltpu.VMEM((16 * PITCH, 128), F32),
                 pltpu.VMEM((rows, kv_width), F32),
                 pltpu.VMEM((rows, kv_width), F32),
+                pltpu.VMEM((2, 16 * GROUP, span), BF16),
+                pltpu.VMEM((2, 16 * GROUP, 128), F32),
                 pltpu.VMEM((groups, BLOCK, 256), F32),
                 pltpu.VMEM((groups // 2, BLOCK, 256), F32),
                 pltpu.VMEM((groups // 4, BLOCK, 256), F32),
@@ -403,14 +497,14 @@
                 pltpu.VMEM((rows // 8, width), F32),
                 pltpu.VMEM((rows, width), F32),
                 pltpu.SemaphoreType.DMA((SLOTS, 2)),
-                pltpu.SemaphoreType.DMA((5,)),
+                pltpu.SemaphoreType.DMA((4 + rows // 128,)),
                 pltpu.SemaphoreType.DMA((n,)),
                 pltpu.SemaphoreType.DMA((n, 10)),
                 pltpu.SemaphoreType.DMA((n, 10)),
             ],
             compiler_params=pltpu.CompilerParams(
                 collective_id=0, has_side_effects=True, vmem_limit_bytes=67043328),
-        )(lengths, lengths.reshape(1, rows), inv_freq, ln_gain.reshape(1, width), ln_bias.reshape(1, width),
+        )(lengths, lengths.reshape(1, rows), inv_freq, ln_gain.reshape(width // 128, 128), ln_bias.reshape(width // 128, 128),
           hidden, w_q, w_k, w_v, w_o, keys, values)
         k_new = jnp.transpose(k_new.reshape(kv_local, head_dim, rows), (2, 0, 1))
         v_new = jnp.transpose(v_new.reshape(kv_local, head_dim, rows), (2, 0, 1))

time: 131 us -> 86.7 us (0.66)
  Pallas kernels: 123 us -> 81.2 us
  local copies, waits for them, and re-layouts: 7.21 us -> 4.63 us
    pallas_call x1, Pallas kernels: 123 us -> 81.2 us  [local_step(): pl.pallas_call(attention_kernel, out_shape=(jax.ShapeDtypeStruct((rows, w...]
    reshape x2 -> x0, local copies, waits for them, and re-layouts: 2.58 us -> none  [the longest x1 1.29 us: local_step(): ln_gain.reshape(1, width)]
where the time goes in v2:
time: 86.7 us; the launch traced here: 86.5 us
  Pallas kernels  81.2 us (94%)
  local copies, waits for them, and re-layouts  4.63 us (5%)
    pallas_call x1, Pallas kernels, local_step(): pl.pallas_call(attention_kernel, out_shape=(jax.ShapeDtypeStruct((rows, w...  81.2 us
    unnamed x7, local copies, waits for them, and re-layouts  4.63 us

profile of v2, /device:TPU:1, one launch (start us, length us, event | category | flops | bytes accessed | tf_op | source)
XLA Modules:
  0.0 86.5 jit_solution(4235092607965378910)
XLA Ops:
  0.6 81.2 %shard_map.130 = (bf16[512,2048]{1,0:T(8,128)(2,1)}, bf16[256,512]{1,0:T(8,128)(2,1)}, bf16[256,512]{1,0:T(8,128)(2,1)}) custom-call(s32[512]{0:T(512)} %len_sm.1, s32[1,512]{1,0:T(1,128)} %bitcast.17, f32[16,128]{1,0:T(8,128)} %constant.2.clone.inv_freq, bf16[16,128]{1,0:T(8,128)(2,1)} %bitcast.18, bf16[16,128]{1,0:T(8,128)(2,1)} %bitcast.19, ...), custom_call_target="tpu_custom_call" | custom-call | tf_op jit(solution)/shard_map/pallas_call | solution.py:467
  81.8 0.0 copy-start.1
  81.8 0.0 copy-start
  81.9 3.2 %copy.17 = bf16[512,2048]{1,0:T(8,128)(2,1)} copy(bf16[512,2048]{1,0:T(8,128)(2,1)} %get-tuple-element.12) | data formatting | bytes 4194304
  85.1 0.0 copy-done.1
  85.1 0.7 copy.18
  85.8 0.0 copy-done
  85.8 0.7 copy.19
Async XLA Ops:
  81.8 3.2 %copy-start.1 = (bf16[256,512]{1,0:T(8,128)(2,1)S(1)}, bf16[256,512]{1,0:T(8,128)(2,1)}, u32[]{:S(2)}) copy-start(bf16[256,512]{1,0:T(8,128)(2,1)} %get-tuple-element.7) | copy-start | bytes 786436
  81.8 3.9 %copy-start = (bf16[256,512]{1,0:T(8,128)(2,1)S(1)}, bf16[256,512]{1,0:T(8,128)(2,1)}, u32[]{:S(2)}) copy-start(bf16[256,512]{1,0:T(8,128)(2,1)} %get-tuple-element.8) | copy-start | bytes 786436

commit v3 on v2

--- a/solution.py
+++ b/solution.py
@@ -1,5 +1,4 @@
 import functools
-import math
 
 import jax
 import jax.numpy as jnp
@@ -17,9 +16,14 @@
 GROUP = 16
 BLOCK = 4 * GROUP + 8
 DIRECT = (3, 4)
-CHUNKS = (8, 8, 8, 4, 4)
+CHUNKS = (8, 8, 4, 4, 4, 4)
+DIRECT = (5,)
+INSIDE = ((3, 0, 1), (4, 0, 2), (7, 1, 1), (8, 1, 2), (8, 0, 3), (9, 2, 1), (10, 1, 3), (10, 2, 2), (11, 0, 4), (11, 3, 1),
+          (12, 2, 3), (12, 3, 2), (12, 1, 4), (13, 4, 1), (14, 4, 2), (14, 0, 5), (14, 3, 3))
+AFTER = ((2, 4), (5, 1), (5, 2), (1, 5), (4, 3), (3, 4), (5, 3), (4, 4), (3, 5), (5, 4), (1, 6), (2, 5), (5, 5), (0, 6), (3, 6),
+         (4, 5), (1, 7), (2, 6), (5, 6), (3, 7), (4, 6), (0, 7), (5, 7), (4, 7), (2, 7))
 SLOTS = 7
-LAGS = (0, 0.9, 2.9, 4.8, 6.8, 7.7, 8.6)
+TALL = 256
 PITCH = 520
 
 
@@ -102,7 +106,7 @@
         load_wk.wait()
         load_wv.wait()
         load_wq.wait()
-    lane_rb = lax.broadcasted_iota(jnp.int32, (128, 128), 1)
+    lane_rb = lax.broadcasted_iota(jnp.int32, (TALL, 128), 1)
     low_half = lane_rb < 64
     first_rot = (lane_rb % 64) < 16
 
@@ -111,8 +115,8 @@
         return (u * cos_b + partner * sin_b).astype(BF16).astype(F32)
 
     def project(i, _):
-        start = pl.multiple_of(i * 128, 128)
-        at = pl.ds(start, 128)
+        start = pl.multiple_of(i * TALL, TALL)
+        at = pl.ds(start, TALL)
         normed = stage[at, :]
         cos_b, sin_b = cos_t[at, :], sin_t[at, :]
         for head in range(4):
@@ -125,8 +129,8 @@
                 else:
                     a, b = jnp.where(low_half, 0.0, swap), jnp.where(low_half, 0.0, u)
                 r = head * 4 + 2 * j
-                qx[pl.ds(pl.multiple_of(r * PITCH + start, 8), 128), :] = a
-                qx[pl.ds(pl.multiple_of((r + 1) * PITCH + start, 8), 128), :] = b
+                qx[pl.ds(pl.multiple_of(r * PITCH + start, 8), TALL), :] = a
+                qx[pl.ds(pl.multiple_of((r + 1) * PITCH + start, 8), TALL), :] = b
         kp = jnp.dot(normed, wk[...], preferred_element_type=F32)
         vp = jnp.dot(normed, wv[...], preferred_element_type=F32)
         for j in range(2):
@@ -140,7 +144,7 @@
         return 0
 
     with jax.named_scope('project'):
-        lax.fori_loop(0, rows // 128, project, 0)
+        lax.fori_loop(0, rows // TALL, project, 0)
     with jax.named_scope('barrier'):
         pl.semaphore_wait(barrier, 4)
 
@@ -305,13 +309,10 @@
         for dx in (1, 0):
             side = x ^ dx
 
-            def body(i, _):
-                out = (send2, mine)[1 - dx]
+            out = (send2, mine)[1 - dx]
+            for i in range(n):
                 merge(own, starts[c] + (core * 2 + side) * n + i, part, starts[c] // 2 + side * n + i,
                       store_to(out, starts[c] // 4 + i, False))
-                return 0
-
-            lax.fori_loop(0, n, body, 0)
             if dx == 1:
                 over_x(c).start()
 
@@ -322,12 +323,9 @@
         with jax.named_scope(f'wait3_{c}'):
             over_x(c).wait_recv()
 
-        def body(i, _):
+        for i in range(n):
             at = starts[c] // 4 + i
             merge(mine, at, recv2, at, store_to(ctx, i, True))
-            return 0
-
-        lax.fori_loop(0, n, body, 0)
         m = n * GROUP
         side = ctx.shape[0] // 2
         lhs = [jnp.concatenate([ctx[pl.ds(t * side + g, m, stride=4), :] for t in range(2)], 1).astype(BF16) for g in range(4)]
@@ -389,8 +387,6 @@
             steps[i](c)
 
     steps = (step1, step2, step3, step4, step5, step6, step7)
-    events = sorted(((starts[c] + CHUNKS[c]) / 2 - 1 + LAGS[i], c, i) for c in range(len(CHUNKS)) for i in range(7))
-
     def wait_for(keys, values):
         for g in keys:
             ring_copy(0, g).wait()
@@ -418,9 +414,8 @@
         refill(1, g)
         refill(0, g + 2)
         refill(1, g + 1)
-        for when, c, k in events:
-            if when <= trips - 1:
-                pl.when(i == math.ceil(when))(functools.partial(scoped, k, c))
+        for when, c, k in INSIDE:
+            pl.when(i == when)(functools.partial(scoped, k - 1, c))
         return 0
 
     trips = groups // 2 - 1
@@ -431,9 +426,8 @@
     with jax.named_scope('attend'):
         attend((last + 1, 1), (last, 0))
         attend(None, (last + 1, 1))
-    for when, c, k in events:
-        if when > trips - 1:
-            scoped(k, c)
+    for c, k in AFTER:
+        scoped(k - 1, c)
     with jax.named_scope('finish'):
         for c in range(len(CHUNKS)):
             to_partner(c).wait_send()
@@ -446,6 +440,26 @@
             for kind, origin in passed:
                 forward(c, kind, origin).wait_send()
             out_copy(c).wait()
+
+
+def copy_kernel(*refs):
+    n = len(refs) // 4
+    sources, results, staged = refs[:n], refs[n:2 * n], refs[2 * n:3 * n]
+    sems = refs[3 * n:]
+    pieces = []
+    for src, dst, mid, sem in zip(sources, results, staged, sems):
+        count = src.shape[0] // 64
+        for i in range(count):
+            at = pl.ds(i * 64, 64)
+            pieces.append((pltpu.make_async_copy(src.at[at], mid.at[at], sem.at[i, 0]),
+                           pltpu.make_async_copy(mid.at[at], dst.at[at], sem.at[i, 1])))
+    for load, _ in pieces:
+        load.start()
+    for load, save in pieces:
+        load.wait()
+        save.start()
+    for _, save in pieces:
+        save.wait()
 
 
 def solution(mesh):
@@ -506,6 +520,16 @@
                 collective_id=0, has_side_effects=True, vmem_limit_bytes=67043328),
         )(lengths, lengths.reshape(1, rows), inv_freq, ln_gain.reshape(width // 128, 128), ln_bias.reshape(width // 128, 128),
           hidden, w_q, w_k, w_v, w_o, keys, values)
+        arrays = (out, k_new, v_new)
+        out, k_new, v_new = pl.pallas_call(
+            copy_kernel,
+            out_shape=[jax.ShapeDtypeStruct(a.shape, a.dtype) for a in arrays],
+            in_specs=[hbm] * 3,
+            out_specs=[hbm] * 3,
+            scratch_shapes=[pltpu.VMEM(a.shape, a.dtype) for a in arrays]
+            + [pltpu.SemaphoreType.DMA((a.shape[0] // 64, 2)) for a in arrays],
+            compiler_params=pltpu.CompilerParams(vmem_limit_bytes=67043328),
+        )(*arrays)
         k_new = jnp.transpose(k_new.reshape(kv_local, head_dim, rows), (2, 0, 1))
         v_new = jnp.transpose(v_new.reshape(kv_local, head_dim, rows), (2, 0, 1))
         return out, k_new, v_new

time: 86.7 us -> 74.7 us (0.86)
  Pallas kernels: 81.2 us -> 73.9 us
  local copies, waits for them, and re-layouts: 4.63 us -> 0 us
    pallas_call x1, Pallas kernels: 81.2 us -> 71.1 us  [local_step(): pl.pallas_call(attention_kernel, out_shape=(jax.ShapeDtypeStruct((rows, w...]
    unnamed x7 -> x0, local copies, waits for them, and re-layouts: 4.63 us -> none
    pallas_call x0 -> x1, Pallas kernels: none -> 2.77 us  [local_step(): pl.pallas_call(copy_kernel, out_shape=[jax.ShapeDtypeStruct(a.shape, a.dt...]
where the time goes in v3:
time: 74.7 us; the launch traced here: 74.5 us
  Pallas kernels  73.9 us (99%)
    pallas_call x1, Pallas kernels, local_step(): pl.pallas_call(attention_kernel, out_shape=(jax.ShapeDtypeStruct((rows, w...  71.1 us
    pallas_call x1, Pallas kernels, local_step(): pl.pallas_call(copy_kernel, out_shape=[jax.ShapeDtypeStruct(a.shape, a.dt...  2.77 us

profile of v3, /device:TPU:1, one launch (start us, length us, event | category | flops | bytes accessed | tf_op | source)
XLA Modules:
  0.0 74.5 jit_solution(16697125207410424296)
XLA Ops:
  0.6 71.1 %shard_map.130 = (bf16[512,2048]{1,0:T(8,128)(2,1)}, bf16[256,512]{1,0:T(8,128)(2,1)}, bf16[256,512]{1,0:T(8,128)(2,1)}) custom-call(s32[512]{0:T(512)} %len_sm.1, s32[1,512]{1,0:T(1,128)} %bitcast.15, f32[16,128]{1,0:T(8,128)} %constant.2.clone.inv_freq, bf16[16,128]{1,0:T(8,128)(2,1)} %bitcast.16, bf16[16,128]{1,0:T(8,128)(2,1)} %bitcast.17, ...), custom_call_target="tpu_custom_call" | custom-call | tf_op jit(solution)/shard_map/pallas_call | solution.py:481
  71.8 2.8 %shard_map.131 = (bf16[512,2048]{1,0:T(8,128)(2,1)}, bf16[256,512]{1,0:T(8,128)(2,1)}, bf16[256,512]{1,0:T(8,128)(2,1)}) custom-call(bf16[512,2048]{1,0:T(8,128)(2,1)} %get-tuple-element.9.refs_0_, bf16[256,512]{1,0:T(8,128)(2,1)} %get-tuple-element.10.refs_1_, bf16[256,512]{1,0:T(8,128)(2,1)} %get-tuple-element.11.refs_2_), custom_call_target="tpu_custom_call" | custom-call | tf_op jit(solution)/shard_map/pallas_call | solution.py:524

commit v4 on v3

--- a/solution.py
+++ b/solution.py
@@ -15,22 +15,25 @@
 
 GROUP = 16
 BLOCK = 4 * GROUP + 8
-DIRECT = (3, 4)
-CHUNKS = (8, 8, 4, 4, 4, 4)
-DIRECT = (5,)
-INSIDE = ((3, 0, 1), (4, 0, 2), (7, 1, 1), (8, 1, 2), (8, 0, 3), (9, 2, 1), (10, 1, 3), (10, 2, 2), (11, 0, 4), (11, 3, 1),
-          (12, 2, 3), (12, 3, 2), (12, 1, 4), (13, 4, 1), (14, 4, 2), (14, 0, 5), (14, 3, 3))
-AFTER = ((2, 4), (5, 1), (5, 2), (1, 5), (4, 3), (3, 4), (5, 3), (4, 4), (3, 5), (5, 4), (1, 6), (2, 5), (5, 5), (0, 6), (3, 6),
-         (4, 5), (1, 7), (2, 6), (5, 6), (3, 7), (4, 6), (0, 7), (5, 7), (4, 7), (2, 7))
+
+CHUNKS = (4, 4, 4, 4, 4, 4, 4, 2, 2)
+DIRECT = (7, 8)
+INSIDE = ((1, 0, 1), (2, 0, 2), (3, 1, 1), (4, 0, 3), (4, 1, 2), (5, 2, 1), (6, 2, 2), (6, 1, 3), (7, 0, 4), (7, 3, 1),
+          (8, 3, 2), (8, 2, 3), (9, 1, 4), (9, 4, 1), (10, 4, 2), (10, 0, 5), (10, 3, 3), (11, 2, 4), (11, 5, 1), (12, 4,
+          3), (12, 5, 2), (13, 2, 5), (13, 3, 4), (13, 6, 1), (14, 6, 2), (14, 4, 4), (14, 5, 3), (14, 7, 1))
+AFTER = ((8, 1), (7, 2), (3, 5), (0, 6), (6, 3), (8, 2), (1, 5), (4, 5), (7, 3), (6, 4), (0, 7), (8, 3), (5, 4), (2, 6),
+         (7, 4), (2, 7), (8, 4), (5, 5), (4, 6), (6, 5), (1, 6), (8, 5), (3, 6), (8, 6), (7, 5), (5, 6), (3, 7), (6, 6),
+         (7, 6), (4, 7), (1, 7), (8, 7), (5, 7), (6, 7), (7, 7))
 SLOTS = 7
 TALL = 256
+STATS = 32
 PITCH = 520
 
 
 def attention_kernel(len_sm, len_row, inv_freq, gain, bias, hid_hbm, wq_hbm, wk_hbm, wv_hbm, wo_hbm, k_hbm, v_hbm,
                      out_hbm, knt_ref, vnt_ref,
                      hid, wq, wk, wv, wo, kring, vring, stage, cos_t, sin_t, qx, kn, vn,
-                     prob, self_w, own, part, send2, mine, recv2, ctx, proj, recv3, total,
+                     prob, self_w, own, part, send2, mine, recv2, ctx, away, keep, recv3, total,
                      ring_sem, load_sem, out_sem, send_sem, recv_sem):
     rows, width = hid.shape
     groups = rows // GROUP
@@ -200,6 +203,9 @@
         cb = part_b[8:, 128:] + self_w[side, 16 * j + 8:16 * j + 16, :] * v_self[:, 128:]
         return ca, cb
 
+    def pair_row(p):
+        return 8 * p if 8 * p < STATS else 8 * p + 8
+
     def attend(score_g, value_g):
         if score_g is not None:
             g, side = score_g
@@ -209,15 +215,16 @@
             if value_g is not None:
                 v, vside = value_g
                 e, o = value(v, vside, 2 * p), value(v, vside, 2 * p + 1)
-                own[v, 8 * p:8 * p + 8, 0:128] = pack(e[0], o[0], low, keep_w)
-                own[v, 8 * p:8 * p + 8, 128:256] = pack(e[1], o[1], low, keep_w)
+                r = pair_row(p)
+                own[v, r:r + 8, 0:128] = pack(e[0], o[0], low, keep_w)
+                own[v, r:r + 8, 128:256] = pack(e[1], o[1], low, keep_w)
             if score_g is not None:
                 e = weigh(g, side, 2 * p, scores[2 * p])
                 o = weigh(g, side, 2 * p + 1, scores[2 * p + 1])
                 tile = jnp.where(pair_of == p, pack(e, o, even, keep_s), tile)
         if score_g is not None:
-            own[g, 4 * GROUP:BLOCK, 0:128] = tile
-            own[g, 4 * GROUP:BLOCK, 128:256] = zero8
+            own[g, STATS:STATS + 8, 0:128] = tile
+            own[g, STATS:STATS + 8, 128:256] = zero8
 
     is_top = stat < 4
 
@@ -225,32 +232,39 @@
         c = p * 8 + 2 * t
         return jnp.where(low, jnp.broadcast_to(f[:, c:c + 1], (8, 128)), jnp.broadcast_to(f[:, c + 1:c + 2], (8, 128)))
 
-    def merge(a_ref, a, b_ref, b, emit):
-        sa, sb = a_ref[a, 4 * GROUP:BLOCK, 0:128], b_ref[b, 4 * GROUP:BLOCK, 0:128]
+    def factors(a_ref, a, b_ref, b):
+        sa, sb = a_ref[a, STATS:STATS + 8, 0:128], b_ref[b, STATS:STATS + 8, 0:128]
         top = jnp.maximum(sa, sb)
         fa, fb = jnp.exp(sa - top), jnp.exp(sb - top)
         denom = sa * pltpu.roll(fa, 4, 1) + sb * pltpu.roll(fb, 4, 1)
-        emit(None, None, jnp.where(is_top, top, denom))
-        for p in range(GROUP // 2):
-            r = slice(8 * p, 8 * p + 8)
+        return fa, fb, denom, jnp.where(is_top, top, denom)
+
+    def pairs(side, values):
+        if side is None:
+            return [pair_row(p) for p in range(GROUP // 2)], values
+        rows_of = [pl.multiple_of((STATS + 8) * side + 8 * p, 8) for p in range(GROUP // 4)]
+        return rows_of, tuple(jnp.where(side == 1, pltpu.roll(f, 96, 1), f) for f in values)
+
+    def blend(a_ref, a, b_ref, b, found, side, out_ref, out):
+        at, (fa, fb) = pairs(side, found[:2])
+        for p, r in enumerate(at):
             for t in range(2):
                 c = slice(t * 128, t * 128 + 128)
-                w = a_ref[a, r, c] * spread(fa, p, t) + b_ref[b, r, c] * spread(fb, p, t)
-                emit(r, c, w / spread(denom, p, 2 + t) if emit.final else w)
-
-    def store_to(ref, index, final):
-        def emit(r, c, value):
-            if r is None:
-                if not final:
-                    ref[index, 4 * GROUP:BLOCK, 0:128] = value
-                    ref[index, 4 * GROUP:BLOCK, 128:256] = zero8
-            elif final:
-                base = c.start // 128 * (ref.shape[0] // 2)
-                ref[pl.ds(pl.multiple_of(base + index * 4 * GROUP + r.start, 8), 8), :] = value
-            else:
-                ref[index, r, c] = value
-        emit.final = final
-        return emit
+                r8 = pl.ds(r, 8)
+                out_ref[out, r8, c] = a_ref[a, r8, c] * spread(fa, p, t) + b_ref[b, r8, c] * spread(fb, p, t)
+        out_ref[out, STATS:STATS + 8, 0:128] = found[3]
+        out_ref[out, STATS:STATS + 8, 128:256] = zero8
+
+    def finish(a_ref, a, b_ref, b, side, unit):
+        found = factors(a_ref, a, b_ref, b)
+        at, (fa, fb, denom) = pairs(side, found[:3])
+        for p, r in enumerate(at):
+            for t in range(2):
+                c = slice(t * 128, t * 128 + 128)
+                r8 = pl.ds(r, 8)
+                w = a_ref[a, r8, c] * spread(fa, p, t) + b_ref[b, r8, c] * spread(fb, p, t)
+                base = t * (ctx.shape[0] // 2) + unit * 4 * GROUP + 8 * p
+                ctx[base:base + 8, :] = w / spread(denom, p, 2 + t)
 
     starts = [sum(CHUNKS[:c]) for c in range(len(CHUNKS))]
 
@@ -259,27 +273,35 @@
             src_ref=src, dst_ref=dst, send_sem=send_sem.at[c, kind], recv_sem=recv_sem.at[c, kind],
             device_id=device(*peer), device_id_type=MESH)
 
-    def quarter(c):
-        return CHUNKS[c] // 4
+    units = [max(n // 4, 1) for n in CHUNKS]
+    blocks_at = [sum(units[:c]) for c in range(len(CHUNKS))]
+    columns = width // 2
+
+    def quarter_rows(c):
+        return CHUNKS[c] * GROUP // 4
+
+    def quarters(c):
+        return pl.ds(starts[c] * GROUP // 4, quarter_rows(c))
 
     def to_partner(c):
-        n = quarter(c)
-        src = own.at[pl.ds(starts[c] + (1 - core) * 2 * n, 2 * n)]
-        return remote(c, 0, src, part.at[pl.ds(starts[c] // 2, 2 * n)], (0, 1, 0))
+        n = CHUNKS[c] // 2
+        src = own.at[pl.ds(starts[c] + (1 - core) * n, n)]
+        return remote(c, 0, src, part.at[pl.ds(starts[c] // 2, n)], (0, 1, 0))
 
     def over_x(c):
-        at = pl.ds(starts[c] // 4, quarter(c))
+        if CHUNKS[c] < 4:
+            at = blocks_at[c], pl.ds(pl.multiple_of(STATS * (1 - x), 8), STATS + 8)
+        else:
+            at = pl.ds(blocks_at[c], units[c])
         return remote(c, 1, send2.at[at], recv2.at[at], (1, 0, 0))
 
     def over_y(c):
-        half = quarter(c) * GROUP // 2
-        src = proj.at[pl.ds(pl.multiple_of(starts[c] // 4 * GROUP + (1 - tp) * half, 8), half)]
-        return remote(c, 2, src, recv3.at[pl.ds(starts[c] // 4 * GROUP // 2, half)], (0, 0, 1))
+        return remote(c, 2, away.at[quarters(c)], recv3.at[quarters(c)], (0, 0, 1))
 
     def home(c, dx, dcore, dtp):
-        half = quarter(c) * GROUP // 2
-        index = ((core ^ dcore) * 2 + (x ^ dx)) * 2 + (tp ^ dtp)
-        return total.at[pl.ds(pl.multiple_of(starts[c] * GROUP + index * half, 8), half)]
+        n = quarter_rows(c)
+        at = pl.ds(pl.multiple_of(starts[c] * GROUP + ((core ^ dcore) * 2 + (x ^ dx)) * n, 8), n)
+        return total.at[at, pl.ds(pl.multiple_of((tp ^ dtp) * columns, columns), columns)]
 
     def spread_own(c, kind, peer):
         return remote(c, kind, home(c, 0, 0, 0), home(c, 0, 0, 0), peer)
@@ -303,49 +325,50 @@
         to_partner(c).start()
 
     def step2(c):
-        n = quarter(c)
+        n = units[c]
         with jax.named_scope(f'wait2_{c}'):
             to_partner(c).wait_recv()
+        work = []
         for dx in (1, 0):
             side = x ^ dx
-
-            out = (send2, mine)[1 - dx]
             for i in range(n):
-                merge(own, starts[c] + (core * 2 + side) * n + i, part, starts[c] // 2 + side * n + i,
-                      store_to(out, starts[c] // 4 + i, False))
-            if dx == 1:
+                if CHUNKS[c] < 4:
+                    a, b, half = starts[c] + core, starts[c] // 2, side
+                else:
+                    a, b, half = starts[c] + (core * 2 + side) * n + i, starts[c] // 2 + side * n + i, None
+                work.append((a, b, half, factors(own, a, part, b), (mine, send2)[dx], blocks_at[c] + i))
+        for k, (a, b, half, found, out_ref, out) in enumerate(work):
+            blend(own, a, part, b, found, half, out_ref, out)
+            if k == n - 1:
                 over_x(c).start()
 
     def step3(c):
-        n = quarter(c)
         if c == 0:
             load_wo.wait()
         with jax.named_scope(f'wait3_{c}'):
             over_x(c).wait_recv()
-
-        for i in range(n):
-            at = starts[c] // 4 + i
-            merge(mine, at, recv2, at, store_to(ctx, i, True))
-        m = n * GROUP
+        for i in range(units[c]):
+            at = blocks_at[c] + i
+            finish(mine, at, recv2, at, x if CHUNKS[c] < 4 else None, i)
+        m = quarter_rows(c)
         side = ctx.shape[0] // 2
         lhs = [jnp.concatenate([ctx[pl.ds(t * side + g, m, stride=4), :] for t in range(2)], 1).astype(BF16) for g in range(4)]
-        for col in range(width // 256):
-            cut = slice(col * 256, col * 256 + 256)
-            acc = None
-            for g in range(4):
-                rhs = jnp.concatenate([wo[h * 256 + g * 64:h * 256 + g * 64 + 64, cut] for h in range(4)], 0)
-                term = jnp.dot(lhs[g], rhs, preferred_element_type=F32)
-                acc = term if acc is None else acc + term
-            proj[starts[c] // 4 * GROUP:starts[c] // 4 * GROUP + m, cut] = acc
-        over_y(c).start()
+        for out_ref, which in ((away, 1 - tp), (keep, tp)):
+            for col in range(columns // 256):
+                cut = pl.ds(pl.multiple_of(which * columns + col * 256, 256), 256)
+                acc = None
+                for g in range(4):
+                    rhs = jnp.concatenate([wo[h * 256 + g * 64:h * 256 + g * 64 + 64, cut] for h in range(4)], 0)
+                    term = jnp.dot(lhs[g], rhs, preferred_element_type=F32)
+                    acc = term if acc is None else acc + term
+                out_ref[quarters(c), col * 256:col * 256 + 256] = acc
+            if out_ref is away:
+                over_y(c).start()
 
     def step4(c):
-        half = quarter(c) * GROUP // 2
         with jax.named_scope(f'wait4_{c}'):
             over_y(c).wait_recv()
-        src = pl.ds(pl.multiple_of(starts[c] // 4 * GROUP + tp * half, 8), half)
-        other = starts[c] // 4 * GROUP // 2
-        home(c, 0, 0, 0)[...] = proj[src, :] + recv3[other:other + half, :]
+        home(c, 0, 0, 0)[...] = keep[quarters(c), :] + recv3[quarters(c), :]
         for copy in sent(c):
             copy.start()
 
@@ -503,12 +526,13 @@
                 pltpu.VMEM((2, 16 * GROUP, 128), F32),
                 pltpu.VMEM((groups, BLOCK, 256), F32),
                 pltpu.VMEM((groups // 2, BLOCK, 256), F32),
-                pltpu.VMEM((groups // 4, BLOCK, 256), F32),
-                pltpu.VMEM((groups // 4, BLOCK, 256), F32),
-                pltpu.VMEM((groups // 4, BLOCK, 256), F32),
+                pltpu.VMEM((sum(max(c // 4, 1) for c in CHUNKS), BLOCK, 256), F32),
+                pltpu.VMEM((sum(max(c // 4, 1) for c in CHUNKS), BLOCK, 256), F32),
+                pltpu.VMEM((sum(max(c // 4, 1) for c in CHUNKS), BLOCK, 256), F32),
                 pltpu.VMEM((2 * (max(CHUNKS) // 4) * GROUP * 4, 128), F32),
-                pltpu.VMEM((rows // 4, width), F32),
-                pltpu.VMEM((rows // 8, width), F32),
+                pltpu.VMEM((rows // 4, width // 2), F32),
+                pltpu.VMEM((rows // 4, width // 2), F32),
+                pltpu.VMEM((rows // 4, width // 2), F32),
                 pltpu.VMEM((rows, width), F32),
                 pltpu.SemaphoreType.DMA((SLOTS, 2)),
                 pltpu.SemaphoreType.DMA((4 + rows // 128,)),

time: 74.7 us -> 73.7 us (0.987)
  Pallas kernels: 73.9 us -> 72.7 us
    pallas_call x1, Pallas kernels: 71.1 us -> 70 us  [local_step(): pl.pallas_call(attention_kernel, out_shape=(jax.ShapeDtypeStruct((rows, w...]
where the time goes in v4:
time: 73.7 us; the launch traced here: 73.5 us
  Pallas kernels  72.7 us (99%)
  between operations  0.8 us (1%)
    pallas_call x1, Pallas kernels, local_step(): pl.pallas_call(attention_kernel, out_shape=(jax.ShapeDtypeStruct((rows, w...  70 us
    pallas_call x1, Pallas kernels, local_step(): pl.pallas_call(copy_kernel, out_shape=[jax.ShapeDtypeStruct(a.shape, a.dt...  2.77 us

profile of v4, /device:TPU:1, one launch (start us, length us, event | category | flops | bytes accessed | tf_op | source)
XLA Modules:
  0.0 73.5 jit_solution(2671629119790809395)
XLA Ops:
  0.6 70.0 %shard_map.130 = (bf16[512,2048]{1,0:T(8,128)(2,1)}, bf16[256,512]{1,0:T(8,128)(2,1)}, bf16[256,512]{1,0:T(8,128)(2,1)}) custom-call(s32[512]{0:T(512)} %len_sm.1, s32[1,512]{1,0:T(1,128)} %bitcast.15, f32[16,128]{1,0:T(8,128)} %constant.2.clone.inv_freq, bf16[16,128]{1,0:T(8,128)(2,1)} %bitcast.16, bf16[16,128]{1,0:T(8,128)(2,1)} %bitcast.17, ...), custom_call_target="tpu_custom_call" | custom-call | tf_op jit(solution)/shard_map/pallas_call | solution.py:504
  70.6 2.8 %shard_map.131 = (bf16[512,2048]{1,0:T(8,128)(2,1)}, bf16[256,512]{1,0:T(8,128)(2,1)}, bf16[256,512]{1,0:T(8,128)(2,1)}) custom-call(bf16[512,2048]{1,0:T(8,128)(2,1)} %get-tuple-element.9.refs_0_, bf16[256,512]{1,0:T(8,128)(2,1)} %get-tuple-element.10.refs_1_, bf16[256,512]{1,0:T(8,128)(2,1)} %get-tuple-element.11.refs_2_), custom_call_target="tpu_custom_call" | custom-call | tf_op jit(solution)/shard_map/pallas_call | solution.py:548

commit v5 on v4

--- a/solution.py
+++ b/solution.py
@@ -1,5 +1,3 @@
-import functools
-
 import jax
 import jax.numpy as jnp
 import numpy as np
@@ -16,23 +14,23 @@
 GROUP = 16
 BLOCK = 4 * GROUP + 8
 
-CHUNKS = (4, 4, 4, 4, 4, 4, 4, 2, 2)
-DIRECT = (7, 8)
-INSIDE = ((1, 0, 1), (2, 0, 2), (3, 1, 1), (4, 0, 3), (4, 1, 2), (5, 2, 1), (6, 2, 2), (6, 1, 3), (7, 0, 4), (7, 3, 1),
-          (8, 3, 2), (8, 2, 3), (9, 1, 4), (9, 4, 1), (10, 4, 2), (10, 0, 5), (10, 3, 3), (11, 2, 4), (11, 5, 1), (12, 4,
-          3), (12, 5, 2), (13, 2, 5), (13, 3, 4), (13, 6, 1), (14, 6, 2), (14, 4, 4), (14, 5, 3), (14, 7, 1))
-AFTER = ((8, 1), (7, 2), (3, 5), (0, 6), (6, 3), (8, 2), (1, 5), (4, 5), (7, 3), (6, 4), (0, 7), (8, 3), (5, 4), (2, 6),
-         (7, 4), (2, 7), (8, 4), (5, 5), (4, 6), (6, 5), (1, 6), (8, 5), (3, 6), (8, 6), (7, 5), (5, 6), (3, 7), (6, 6),
-         (7, 6), (4, 7), (1, 7), (8, 7), (5, 7), (6, 7), (7, 7))
+CHUNKS = (8, 4, 4, 4, 4, 4, 2, 2)
+DIRECT = (7,)
+INSIDE = ((3, 0, 1), (4, 0, 2), (5, 1, 1), (6, 1, 2), (7, 0, 3), (7, 2, 1), (8, 2, 2), (8, 1, 3), (9, 0, 4), (9, 3, 1),
+          (10, 2, 3), (10, 3, 2), (10, 1, 4), (11, 4, 1), (12, 0, 5), (12, 4, 2), (12, 3, 3), (13, 2, 4), (13, 1, 5), (13,
+          5, 1), (14, 5, 2), (14, 3, 4), (14, 6, 1))
+AFTER = ((2, 5), (7, 1), (4, 3), (6, 2), (7, 2), (5, 3), (3, 5), (4, 4), (6, 3), (7, 3), (3, 6), (5, 4), (2, 6), (0, 6),
+         (4, 5), (3, 7), (6, 4), (2, 7), (7, 4), (1, 6), (5, 5), (6, 5), (4, 6), (1, 7), (4, 7), (0, 7), (7, 5), (7, 6),
+         (5, 6), (6, 6), (7, 7), (5, 7), (6, 7))
 SLOTS = 7
 TALL = 256
 STATS = 32
 PITCH = 520
 
 
-def attention_kernel(len_sm, len_row, inv_freq, gain, bias, hid_hbm, wq_hbm, wk_hbm, wv_hbm, wo_hbm, k_hbm, v_hbm,
+def attention_kernel(len_hbm, len_row_hbm, inv_freq_hbm, gain_hbm, bias_hbm, hid_hbm, wq_hbm, wk_hbm, wv_hbm, wo_hbm, k_hbm, v_hbm,
                      out_hbm, knt_ref, vnt_ref,
-                     hid, wq, wk, wv, wo, kring, vring, stage, cos_t, sin_t, qx, kn, vn,
+                     len_sm, len_row, inv_freq, gain, bias, hid, wq, wk, wv, wo, kring, vring, stage, cos_t, sin_t, qx, kn, vn,
                      prob, self_w, own, part, send2, mine, recv2, ctx, away, keep, recv3, total,
                      ring_sem, load_sem, out_sem, send_sem, recv_sem):
     rows, width = hid.shape
@@ -57,6 +55,10 @@
     load_wv = pltpu.make_async_copy(wv_hbm, wv, load_sem.at[1])
     load_wq = pltpu.make_async_copy(wq_hbm, wq, load_sem.at[2])
     load_wo = pltpu.make_async_copy(wo_hbm, wo, load_sem.at[3])
+    small = [pltpu.make_async_copy(src, dst, load_sem.at[4 + blocks + i]) for i, (src, dst) in enumerate(
+        ((len_row_hbm, len_row), (inv_freq_hbm, inv_freq), (gain_hbm, gain), (bias_hbm, bias), (len_hbm, len_sm)))]
+    for copy in small:
+        copy.start()
     for i in range(blocks):
         load_hid(i).start()
     load_wq.start()
@@ -72,6 +74,8 @@
     for peer in ((0, 1, 0), (1, 0, 0), (0, 0, 1), (1, 0, 1)):
         pl.semaphore_signal(barrier, inc=1, device_id=device(*peer), device_id_type=MESH)
 
+    for copy in small:
+        copy.wait()
     angle = inv_freq[:, 0:1] * len_row[0:1, :].astype(F32)
     cos_a, sin_a = jnp.cos(angle), jnp.sin(angle)
     one, zero = jnp.ones((32, rows), F32), jnp.zeros((32, rows), F32)
@@ -82,13 +86,6 @@
         cos_t[cut, :] = cos_full[:, cut].T
         sin_t[cut, :] = sin_full[:, cut].T
 
-    with jax.named_scope('load_hid'):
-        for i in range(blocks):
-            load_hid(i).wait()
-    for g in range(1, SLOTS):
-        for which in range(2):
-            ring_copy(which, g).start()
-    load_wo.start()
     gain_f, bias_f = gain[...].astype(F32), bias[...].astype(F32)
     gain_f = 1.0 + jnp.concatenate([gain_f[i:i + 1] for i in range(width // 128)], 1)
     bias_f = jnp.concatenate([bias_f[i:i + 1] for i in range(width // 128)], 1)
@@ -102,8 +99,16 @@
             stage[at, :] = (centred * lax.rsqrt(var + 1e-5) * gain_f + bias_f).astype(BF16)
         return 0
 
-    with jax.named_scope('norm'):
-        lax.fori_loop(0, rows // 64, norm, 0)
+    for i in range(blocks):
+        with jax.named_scope(f'load_hid{i}'):
+            load_hid(i).wait()
+        if i == 1:
+            for g in range(1, SLOTS):
+                for which in range(2):
+                    ring_copy(which, g).start()
+            load_wo.start()
+        with jax.named_scope('norm'):
+            lax.fori_loop(2 * i, 2 * i + 2, norm, 0)
 
     with jax.named_scope('load_w'):
         load_wk.wait()
@@ -437,8 +442,12 @@
         refill(1, g)
         refill(0, g + 2)
         refill(1, g + 1)
-        for when, c, k in INSIDE:
-            pl.when(i == when)(functools.partial(scoped, k - 1, c))
+        for when in sorted({e[0] for e in INSIDE}):
+            @pl.when(i == when)
+            def _():
+                for at, c, k in INSIDE:
+                    if at == when:
+                        scoped(k - 1, c)
         return 0
 
     trips = groups // 2 - 1
@@ -498,7 +507,6 @@
         inv_freq = np.power(10000.0, -2.0 * np.arange(half_rot) / (2 * half_rot)).astype(np.float32)
         inv_freq = jnp.asarray(np.broadcast_to(inv_freq[:, None], (half_rot, 128)).copy())
         vmem = pl.BlockSpec(memory_space=pltpu.VMEM)
-        smem = pl.BlockSpec(memory_space=pltpu.SMEM)
         hbm = pl.BlockSpec(memory_space=pl.ANY)
         n = len(CHUNKS)
         out, k_new, v_new = pl.pallas_call(
@@ -506,9 +514,14 @@
             out_shape=(jax.ShapeDtypeStruct((rows, width), BF16),
                        jax.ShapeDtypeStruct((kv_width, rows), BF16),
                        jax.ShapeDtypeStruct((kv_width, rows), BF16)),
-            in_specs=[smem, vmem, vmem, vmem, vmem] + [hbm] * 7,
+            in_specs=[hbm] * 12,
             out_specs=(hbm, vmem, vmem),
             scratch_shapes=[
+                pltpu.SMEM((rows,), jnp.int32),
+                pltpu.VMEM((1, rows), jnp.int32),
+                pltpu.VMEM((half_rot, 128), F32),
+                pltpu.VMEM((width // 128, 128), BF16),
+                pltpu.VMEM((width // 128, 128), BF16),
                 pltpu.VMEM((rows, width), BF16),
                 pltpu.VMEM((width, q_width), BF16),
                 pltpu.VMEM((width, kv_width), BF16),
@@ -535,7 +548,7 @@
                 pltpu.VMEM((rows // 4, width // 2), F32),
                 pltpu.VMEM((rows, width), F32),
                 pltpu.SemaphoreType.DMA((SLOTS, 2)),
-                pltpu.SemaphoreType.DMA((4 + rows // 128,)),
+                pltpu.SemaphoreType.DMA((9 + rows // 128,)),
                 pltpu.SemaphoreType.DMA((n,)),
                 pltpu.SemaphoreType.DMA((n, 10)),
                 pltpu.SemaphoreType.DMA((n, 10)),

time: 73.7 us -> 72.6 us (0.985)
  Pallas kernels: 72.7 us -> 71.7 us
    pallas_call x1, Pallas kernels: 70 us -> 68.9 us  [local_step(): pl.pallas_call(attention_kernel, out_shape=(jax.ShapeDtypeStruct((rows, w...]
where the time goes in v5:
time: 72.6 us; the launch traced here: 72.5 us
  Pallas kernels  71.7 us (99%)
  between operations  0.8 us (1%)
    pallas_call x1, Pallas kernels, local_step(): pl.pallas_call(attention_kernel, out_shape=(jax.ShapeDtypeStruct((rows, w...  68.9 us
    pallas_call x1, Pallas kernels, local_step(): pl.pallas_call(copy_kernel, out_shape=[jax.ShapeDtypeStruct(a.shape, a.dt...  2.77 us

profile of v5, /device:TPU:1, one launch (start us, length us, event | category | flops | bytes accessed | tf_op | source)
XLA Modules:
  0.0 72.5 jit_solution(8785727081272676373)
XLA Ops:
  0.6 68.9 %shard_map.130 = (bf16[512,2048]{1,0:T(8,128)(2,1)}, bf16[256,512]{1,0:T(8,128)(2,1)}, bf16[256,512]{1,0:T(8,128)(2,1)}) custom-call(s32[512]{0:T(512)} %len_hbm.1, s32[1,512]{1,0:T(1,128)} %bitcast.15, f32[16,128]{1,0:T(8,128)} %constant.2.clone.inv_freq_hbm, bf16[16,128]{1,0:T(8,128)(2,1)} %bitcast.16, bf16[16,128]{1,0:T(8,128)(2,1)} %bitcast.17, ...), custom_call_target="tpu_custom_call" | custom-call | tf_op jit(solution)/shard_map/pallas_call | solution.py:512
  69.6 2.8 %shard_map.131 = (bf16[512,2048]{1,0:T(8,128)(2,1)}, bf16[256,512]{1,0:T(8,128)(2,1)}, bf16[256,512]{1,0:T(8,128)(2,1)}) custom-call(bf16[512,2048]{1,0:T(8,128)(2,1)} %get-tuple-element.9.refs_0_, bf16[256,512]{1,0:T(8,128)(2,1)} %get-tuple-element.10.refs_1_, bf16[256,512]{1,0:T(8,128)(2,1)} %get-tuple-element.11.refs_2_), custom_call_target="tpu_custom_call" | custom-call | tf_op jit(solution)/shard_map/pallas_call | solution.py:561

commit v6 on v5

--- a/solution.py
+++ b/solution.py
@@ -29,8 +29,8 @@
 
 
 def attention_kernel(len_hbm, len_row_hbm, inv_freq_hbm, gain_hbm, bias_hbm, hid_hbm, wq_hbm, wk_hbm, wv_hbm, wo_hbm, k_hbm, v_hbm,
-                     out_hbm, knt_ref, vnt_ref,
-                     len_sm, len_row, inv_freq, gain, bias, hid, wq, wk, wv, wo, kring, vring, stage, cos_t, sin_t, qx, kn, vn,
+                     out_hbm, knt_hbm, vnt_hbm,
+                     knt_ref, vnt_ref, len_sm, len_row, inv_freq, gain, bias, hid, wq, wk, wv, wo, kring, vring, stage, cos_t, sin_t, qx, kn, vn,
                      prob, self_w, own, part, send2, mine, recv2, ctx, away, keep, recv3, total,
                      ring_sem, load_sem, out_sem, send_sem, recv_sem):
     rows, width = hid.shape
@@ -153,6 +153,10 @@
 
     with jax.named_scope('project'):
         lax.fori_loop(0, rows // TALL, project, 0)
+    new_copies = [pltpu.make_async_copy(src, dst, load_sem.at[4 + blocks + i]) for i, (src, dst) in enumerate(
+        ((knt_ref, knt_hbm), (vnt_ref, vnt_hbm)))]
+    for copy in new_copies:
+        copy.start()
     with jax.named_scope('barrier'):
         pl.semaphore_wait(barrier, 4)
 
@@ -273,9 +277,11 @@
 
     starts = [sum(CHUNKS[:c]) for c in range(len(CHUNKS))]
 
-    def remote(c, kind, src, dst, peer):
+    def remote(c, kind, src, dst, peer, arrival=None):
+        sem = {0: 0, 1: 9 + c}[kind] if isinstance(kind, int) and kind < 2 else kind - 1
         return pltpu.make_async_remote_copy(
-            src_ref=src, dst_ref=dst, send_sem=send_sem.at[c, kind], recv_sem=recv_sem.at[c, kind],
+            src_ref=src, dst_ref=dst, send_sem=send_sem.at[sem],
+            recv_sem=recv_sem.at[c, kind if arrival is None else arrival],
             device_id=device(*peer), device_id_type=MESH)
 
     units = [max(n // 4, 1) for n in CHUNKS]
@@ -312,9 +318,8 @@
         return remote(c, kind, home(c, 0, 0, 0), home(c, 0, 0, 0), peer)
 
     def forward(c, kind, origin):
-        return remote(c, kind, home(c, *origin), home(c, *origin), (0, 1, 0))
-
-    passed = ((7, (1, 0, 0)), (8, (0, 0, 1)), (9, (1, 0, 1)))
+        return remote(c, kind, home(c, *origin), home(c, *origin), (0, 1, 0), 3)
+
     first_peer, other_peer = (1 - core, 0, core), (core, 0, 1 - core)
 
     def sent(c):
@@ -398,9 +403,8 @@
 
     def step7(c):
         with jax.named_scope(f'wait7_{c}'):
-            spread_own(c, 3, (0, 1, 0)).wait_recv()
-            for kind, origin in passed:
-                forward(c, kind, origin).wait_recv()
+            four = total.at[pl.ds(starts[c] * GROUP, CHUNKS[c] * GROUP), pl.ds(0, columns)]
+            remote(c, 3, four, four, (0, 1, 0)).wait_recv()
 
         def body(i, _):
             at = pl.ds(pl.multiple_of((starts[c] + i) * GROUP, GROUP), GROUP)
@@ -461,17 +465,14 @@
     for c, k in AFTER:
         scoped(k - 1, c)
     with jax.named_scope('finish'):
+        remote(0, 0, part, part, (0, 1, 0)).wait_send()
+        for kind in range(2, 10):
+            remote(0, kind, away, away, (0, 1, 0), 3).wait_send()
         for c in range(len(CHUNKS)):
-            to_partner(c).wait_send()
             over_x(c).wait_send()
-            over_y(c).wait_send()
-            for copy in sent(c):
-                copy.wait_send()
-            if c not in DIRECT:
-                relay(c).wait_send()
-            for kind, origin in passed:
-                forward(c, kind, origin).wait_send()
             out_copy(c).wait()
+        for copy in new_copies:
+            copy.wait()
 
 
 def copy_kernel(*refs):
@@ -515,8 +516,10 @@
                        jax.ShapeDtypeStruct((kv_width, rows), BF16),
                        jax.ShapeDtypeStruct((kv_width, rows), BF16)),
             in_specs=[hbm] * 12,
-            out_specs=(hbm, vmem, vmem),
+            out_specs=(hbm, hbm, hbm),
             scratch_shapes=[
+                pltpu.VMEM((kv_width, rows), BF16),
+                pltpu.VMEM((kv_width, rows), BF16),
                 pltpu.SMEM((rows,), jnp.int32),
                 pltpu.VMEM((1, rows), jnp.int32),
                 pltpu.VMEM((half_rot, 128), F32),
@@ -550,8 +553,8 @@
                 pltpu.SemaphoreType.DMA((SLOTS, 2)),
                 pltpu.SemaphoreType.DMA((9 + rows // 128,)),
                 pltpu.SemaphoreType.DMA((n,)),
-                pltpu.SemaphoreType.DMA((n, 10)),
-                pltpu.SemaphoreType.DMA((n, 10)),
+                pltpu.SemaphoreType.DMA((9 + n,)),
+                pltpu.SemaphoreType.DMA((n, 7)),
             ],
             compiler_params=pltpu.CompilerParams(
                 collective_id=0, has_side_effects=True, vmem_limit_bytes=67043328),

time: 72.6 us -> 71.2 us (0.981)
  Pallas kernels: 71.7 us -> 70.3 us
    pallas_call x1, Pallas kernels: 68.9 us -> 67.5 us  [local_step(): pl.pallas_call(attention_kernel, out_shape=(jax.ShapeDtypeStruct((rows, w...]
where the time goes in v6:
time: 71.2 us; the launch traced here: 71.1 us
  Pallas kernels  70.3 us (99%)
  between operations  0.8 us (1%)
    pallas_call x1, Pallas kernels, local_step(): pl.pallas_call(attention_kernel, out_shape=(jax.ShapeDtypeStruct((rows, w...  67.5 us
    pallas_call x1, Pallas kernels, local_step(): pl.pallas_call(copy_kernel, out_shape=[jax.ShapeDtypeStruct(a.shape, a.dt...  2.77 us

profile of v6, /device:TPU:1, one launch (start us, length us, event | category | flops | bytes accessed | tf_op | source)
XLA Modules:
  0.0 71.1 jit_solution(12182582299992144144)
XLA Ops:
  0.6 67.5 %shard_map.130 = (bf16[512,2048]{1,0:T(8,128)(2,1)}, bf16[256,512]{1,0:T(8,128)(2,1)}, bf16[256,512]{1,0:T(8,128)(2,1)}) custom-call(s32[512]{0:T(512)} %len_hbm.1, s32[1,512]{1,0:T(1,128)} %bitcast.15, f32[16,128]{1,0:T(8,128)} %constant.2.clone.inv_freq_hbm, bf16[16,128]{1,0:T(8,128)(2,1)} %bitcast.16, bf16[16,128]{1,0:T(8,128)(2,1)} %bitcast.17, ...), custom_call_target="tpu_custom_call" | custom-call | tf_op jit(solution)/shard_map/pallas_call | solution.py:513
  68.2 2.8 %shard_map.131 = (bf16[512,2048]{1,0:T(8,128)(2,1)}, bf16[256,512]{1,0:T(8,128)(2,1)}, bf16[256,512]{1,0:T(8,128)(2,1)}) custom-call(bf16[512,2048]{1,0:T(8,128)(2,1)} %get-tuple-element.9.refs_0_, bf16[256,512]{1,0:T(8,128)(2,1)} %get-tuple-element.10.refs_1_, bf16[256,512]{1,0:T(8,128)(2,1)} %get-tuple-element.11.refs_2_), custom_call_target="tpu_custom_call" | custom-call | tf_op jit(solution)/shard_map/pallas_call | solution.py:564

commit v7 on v6

--- a/solution.py
+++ b/solution.py
@@ -54,7 +54,11 @@
     load_wk = pltpu.make_async_copy(wk_hbm, wk, load_sem.at[0])
     load_wv = pltpu.make_async_copy(wv_hbm, wv, load_sem.at[1])
     load_wq = pltpu.make_async_copy(wq_hbm, wq, load_sem.at[2])
-    load_wo = pltpu.make_async_copy(wo_hbm, wo, load_sem.at[3])
+
+    def load_wo(i):
+        at = pl.ds(i * (wo.shape[0] // 2), wo.shape[0] // 2)
+        return pltpu.make_async_copy(wo_hbm.at[at], wo.at[at], load_sem.at[(3, 8 + blocks)[i]])
+
     small = [pltpu.make_async_copy(src, dst, load_sem.at[4 + blocks + i]) for i, (src, dst) in enumerate(
         ((len_row_hbm, len_row), (inv_freq_hbm, inv_freq), (gain_hbm, gain), (bias_hbm, bias), (len_hbm, len_sm)))]
     for copy in small:
@@ -64,8 +68,6 @@
     load_wq.start()
     load_wk.start()
     load_wv.start()
-    for which in range(2):
-        ring_copy(which, 0).start()
 
     def device(dx, dcore, dtp):
         return {'sp': (x ^ dx) * 2 + (core ^ dcore), 'tp': tp ^ dtp}
@@ -102,11 +104,10 @@
     for i in range(blocks):
         with jax.named_scope(f'load_hid{i}'):
             load_hid(i).wait()
-        if i == 1:
-            for g in range(1, SLOTS):
+        if i in (1, 3):
+            for g in (range(1), range(1, SLOTS))[i // 2]:
                 for which in range(2):
                     ring_copy(which, g).start()
-            load_wo.start()
         with jax.named_scope('norm'):
             lax.fori_loop(2 * i, 2 * i + 2, norm, 0)
 
@@ -354,7 +355,8 @@
 
     def step3(c):
         if c == 0:
-            load_wo.wait()
+            load_wo(0).wait()
+            load_wo(1).wait()
         with jax.named_scope(f'wait3_{c}'):
             over_x(c).wait_recv()
         for i in range(units[c]):
@@ -446,6 +448,11 @@
         refill(1, g)
         refill(0, g + 2)
         refill(1, g + 1)
+        @pl.when(i == 3)
+        def _():
+            load_wo(0).start()
+            load_wo(1).start()
+
         for when in sorted({e[0] for e in INSIDE}):
             @pl.when(i == when)
             def _():

time: 71.2 us -> 71.2 us (level)
  no operation moved by 1% of the time
where the time goes in v7:
time: 71.2 us; the launch traced here: 71.1 us
  Pallas kernels  70.3 us (99%)
  between operations  0.8 us (1%)
    pallas_call x1, Pallas kernels, local_step(): pl.pallas_call(attention_kernel, out_shape=(jax.ShapeDtypeStruct((rows, w...  67.5 us
    pallas_call x1, Pallas kernels, local_step(): pl.pallas_call(copy_kernel, out_shape=[jax.ShapeDtypeStruct(a.shape, a.dt...  2.77 us

profile of v7, /device:TPU:1, one launch (start us, length us, event | category | flops | bytes accessed | tf_op | source)
XLA Modules:
  0.0 71.1 jit_solution(15318288942977183896)
XLA Ops:
  0.6 67.5 %shard_map.130 = (bf16[512,2048]{1,0:T(8,128)(2,1)}, bf16[256,512]{1,0:T(8,128)(2,1)}, bf16[256,512]{1,0:T(8,128)(2,1)}) custom-call(s32[512]{0:T(512)} %len_hbm.1, s32[1,512]{1,0:T(1,128)} %bitcast.15, f32[16,128]{1,0:T(8,128)} %constant.2.clone.inv_freq_hbm, bf16[16,128]{1,0:T(8,128)(2,1)} %bitcast.16, bf16[16,128]{1,0:T(8,128)(2,1)} %bitcast.17, ...), custom_call_target="tpu_custom_call" | custom-call | tf_op jit(solution)/shard_map/pallas_call | solution.py:520
  68.2 2.8 %shard_map.131 = (bf16[512,2048]{1,0:T(8,128)(2,1)}, bf16[256,512]{1,0:T(8,128)(2,1)}, bf16[256,512]{1,0:T(8,128)(2,1)}) custom-call(bf16[512,2048]{1,0:T(8,128)(2,1)} %get-tuple-element.9.refs_0_, bf16[256,512]{1,0:T(8,128)(2,1)} %get-tuple-element.10.refs_1_, bf16[256,512]{1,0:T(8,128)(2,1)} %get-tuple-element.11.refs_2_), custom_call_target="tpu_custom_call" | custom-call | tf_op jit(solution)/shard_map/pallas_call | solution.py:571

commit v8 on v7

--- a/solution.py
+++ b/solution.py
@@ -16,12 +16,12 @@
 
 CHUNKS = (8, 4, 4, 4, 4, 4, 2, 2)
 DIRECT = (7,)
-INSIDE = ((3, 0, 1), (4, 0, 2), (5, 1, 1), (6, 1, 2), (7, 0, 3), (7, 2, 1), (8, 2, 2), (8, 1, 3), (9, 0, 4), (9, 3, 1),
-          (10, 2, 3), (10, 3, 2), (10, 1, 4), (11, 4, 1), (12, 0, 5), (12, 4, 2), (12, 3, 3), (13, 2, 4), (13, 1, 5), (13,
-          5, 1), (14, 5, 2), (14, 3, 4), (14, 6, 1))
-AFTER = ((2, 5), (7, 1), (4, 3), (6, 2), (7, 2), (5, 3), (3, 5), (4, 4), (6, 3), (7, 3), (3, 6), (5, 4), (2, 6), (0, 6),
-         (4, 5), (3, 7), (6, 4), (2, 7), (7, 4), (1, 6), (5, 5), (6, 5), (4, 6), (1, 7), (4, 7), (0, 7), (7, 5), (7, 6),
-         (5, 6), (6, 6), (7, 7), (5, 7), (6, 7))
+INSIDE = ((3, 0, 1), (4, 0, 2), (5, 1, 1), (6, 0, 3), (6, 1, 2), (7, 2, 1), (8, 2, 2), (8, 1, 3), (8, 0, 4), (9, 3, 1),
+          (10, 3, 2), (10, 2, 3), (10, 0, 5), (10, 1, 4), (11, 3, 3), (11, 2, 4), (11, 4, 1), (12, 4, 2), (12, 0, 6), (13,
+          3, 4), (13, 1, 5), (13, 5, 1), (14, 5, 2), (14, 2, 5), (14, 6, 1))
+AFTER = ((3, 5), (7, 1), (4, 3), (6, 2), (7, 2), (5, 3), (3, 6), (1, 6), (4, 4), (6, 3), (7, 3), (2, 6), (5, 4), (1, 7),
+         (6, 4), (7, 4), (4, 5), (5, 5), (2, 7), (3, 7), (6, 5), (4, 6), (7, 5), (7, 6), (5, 6), (6, 6), (0, 7), (4, 7),
+         (5, 7), (6, 7), (7, 7))
 SLOTS = 7
 TALL = 256
 STATS = 32

time: 71.2 us -> 70.6 us (level)
  Pallas kernels: 70.3 us -> 69.5 us
    pallas_call x1, Pallas kernels: 67.5 us -> 66.8 us  [local_step(): pl.pallas_call(attention_kernel, out_shape=(jax.ShapeDtypeStruct((rows, w...]
where the time goes in v8:
time: 70.6 us; the launch traced here: 70.3 us
  Pallas kernels  69.5 us (98%)
  between operations  0.8 us (1%)
    pallas_call x1, Pallas kernels, local_step(): pl.pallas_call(attention_kernel, out_shape=(jax.ShapeDtypeStruct((rows, w...  66.8 us
    pallas_call x1, Pallas kernels, local_step(): pl.pallas_call(copy_kernel, out_shape=[jax.ShapeDtypeStruct(a.shape, a.dt...  2.77 us

profile of v8, /device:TPU:1, one launch (start us, length us, event | category | flops | bytes accessed | tf_op | source)
XLA Modules:
  0.0 70.3 jit_solution(9331863733336225377)
XLA Ops:
  0.6 66.8 %shard_map.130 = (bf16[512,2048]{1,0:T(8,128)(2,1)}, bf16[256,512]{1,0:T(8,128)(2,1)}, bf16[256,512]{1,0:T(8,128)(2,1)}) custom-call(s32[512]{0:T(512)} %len_hbm.1, s32[1,512]{1,0:T(1,128)} %bitcast.15, f32[16,128]{1,0:T(8,128)} %constant.2.clone.inv_freq_hbm, bf16[16,128]{1,0:T(8,128)(2,1)} %bitcast.16, bf16[16,128]{1,0:T(8,128)(2,1)} %bitcast.17, ...), custom_call_target="tpu_custom_call" | custom-call | tf_op jit(solution)/shard_map/pallas_call | solution.py:520
  67.4 2.8 %shard_map.131 = (bf16[512,2048]{1,0:T(8,128)(2,1)}, bf16[256,512]{1,0:T(8,128)(2,1)}, bf16[256,512]{1,0:T(8,128)(2,1)}) custom-call(bf16[512,2048]{1,0:T(8,128)(2,1)} %get-tuple-element.9.refs_0_, bf16[256,512]{1,0:T(8,128)(2,1)} %get-tuple-element.10.refs_1_, bf16[256,512]{1,0:T(8,128)(2,1)} %get-tuple-element.11.refs_2_), custom_call_target="tpu_custom_call" | custom-call | tf_op jit(solution)/shard_map/pallas_call | solution.py:571
